TPU v7x, 32 devices: a whole 2x2x4 slice. The times are simulated.
32 devices in a mesh: tm: 4 (over y, x), space: 8 (over z, core).
Axes of the slice: x: 2, y: 2, z: 4, core: 2. Of those that a mesh axis runs over, the one named last changes fastest.
Arguments:
- initial_state: float32 [3, 192, 256], P(None, 'space'), may hold values from -2 to 2
- c_guess: float32 [4, 3, 192, 256], P('tm', None, 'space'), may hold values from -2 to 2
- friction: float32 [192, 256], P('space'), may hold values from 0.05 to 1
Outputs:
- c_points: float32 [4, 3, 192, 256], P('tm', None, 'space')
- f_points: float32 [4, 3, 192, 256], P('tm', None, 'space')
All inputs are finite; a program needn't handle non-finite values.
Results may differ from a plain program's by a relative error of at most 0.00012.
Values sent between devices are 32-bit elements; how exact they have to be, the bound alone decides.
No kernel may reach another device: no remote copies, remote signals or barrier semaphores. Data moves between devices by JAX's collectives and lax.ppermute only.
A program may use at most 64 MiB of HBM per device.

v0:
```python
import jax
import jax.numpy as jnp
from jax import lax
from jax.sharding import PartitionSpec as P

STEPS = 8


gravity = 2.0
coriolis = 0.5
viscosity = 0.5
time_step = 0.04


def with_halo(block, sides, width):
    for axis, dim in sides:
        count = lax.axis_size(axis)
        forward = [(i, i + 1) for i in range(count - 1)]
        forward.append((count - 1, 0))
        backward = [(target, source) for source, target in forward]
        low = lax.ppermute(
            lax.slice_in_dim(block, block.shape[dim] - width, None, axis=dim), axis, forward
        )
        high = lax.ppermute(lax.slice_in_dim(block, 0, width, axis=dim), axis, backward)
        block = jnp.concatenate([low, block, high], axis=dim)
    return block


def shifted(value, axis, by):
    size = lax.axis_size(axis)
    pairs = [(i, i + by) for i in range(size) if 0 <= i + by < size]
    return lax.ppermute(value, axis, pairs)


def cut_neighbours(field):
    return (
        field[2:],
        field[:-2],
        jnp.roll(field, -1, 1)[1:-1],
        jnp.roll(field, 1, 1)[1:-1],
        field[1:-1],
    )


def spread(near):
    return near[0] + near[1] + near[2] + near[3] - 4.0 * near[4]


def tendency(fields, drag, neighbours):
    height = fields[0]
    row_vel = fields[1]
    col_vel = fields[2]
    height_near = neighbours(height)
    row_near = neighbours(row_vel)
    col_near = neighbours(col_vel)
    flux_row = neighbours((1.0 + height) * row_vel)
    flux_col = neighbours((1.0 + height) * col_vel)
    row_mid = row_near[4]
    col_mid = col_near[4]
    rate_height = -(
        0.5 * (flux_row[0] - flux_row[1]) + 0.5 * (flux_col[2] - flux_col[3])
    ) + viscosity * spread(height_near)
    rate_row = (
        -(
            row_mid * (0.5 * (row_near[0] - row_near[1]))
            + col_mid * (0.5 * (row_near[2] - row_near[3]))
        )
        - gravity * (0.5 * (height_near[0] - height_near[1]))
        + coriolis * col_mid
        - drag * row_mid
        + viscosity * spread(row_near)
    )
    rate_col = (
        -(
            row_mid * (0.5 * (col_near[0] - col_near[1]))
            + col_mid * (0.5 * (col_near[2] - col_near[3]))
        )
        - gravity * (0.5 * (height_near[2] - height_near[3]))
        - coriolis * row_mid
        - drag * col_mid
        + viscosity * spread(col_near)
    )
    return jnp.stack([rate_height, rate_row, rate_col])


def trim_rows(array, width):
    return array[..., width : array.shape[-2] - width, :]


def heun_step(fields, drag, size):
    slope_one = tendency(fields, drag[1:-1], cut_neighbours)
    midpoint = fields[:, 1:-1] + size * slope_one
    slope_two = tendency(midpoint, drag[2:-2], cut_neighbours)
    return fields[:, 2:-2] + 0.5 * size * (slope_one[:, 1:-1] + slope_two)


def advance(fields, drag_pad, step_count, layers, with_coarse):
    coarse = fields
    reaches = [layers] * (step_count // layers)
    if step_count % layers:
        reaches = reaches + [step_count % layers]
    for group, reach in enumerate(reaches):
        padded = with_halo(fields, (("space", 1),), 2 * reach)
        drag = trim_rows(drag_pad, 8 - 2 * reach)
        if with_coarse and group == 0:
            coarse = trim_rows(heun_step(padded, drag, STEPS * time_step), 2 * reach - 2)
        for repeat in range(reach):
            padded = heun_step(padded, drag, time_step)
            drag = trim_rows(drag, 2)
        fields = padded
    return (fields, coarse)


def body(initial_state, c_guess, friction):
    slice_index = lax.axis_index("tm")
    coarse_step = STEPS * time_step
    layers = 4
    drag_pad = with_halo(friction, (("space", 0),), 8)

    def earlier(fields):
        incoming = shifted(fields, "tm", 1)
        return jnp.where(slice_index == 0, initial_state, incoming)

    relaxed, unused = advance(earlier(c_guess[0]), drag_pad, STEPS, layers, False)
    fine_end, coarse_end = advance(earlier(relaxed), drag_pad, STEPS, layers, True)
    defect = fine_end - coarse_end
    defect_pad = with_halo(defect, (("space", 1),), 8)
    gathered = lax.all_gather(defect_pad[None], "tm", axis=0, tiled=True)

    def group_fn(group, carry):
        current, owned = carry
        padded = with_halo(current, (("space", 1),), 8)
        drag = drag_pad
        for offset in range(4):
            turn = group * 4 + offset
            defect_now = trim_rows(
                lax.dynamic_index_in_dim(gathered, turn, 0, keepdims=False), 2 * offset + 2
            )
            padded = heun_step(padded, drag, coarse_step) + defect_now
            drag = trim_rows(drag, 2)
            owned = jnp.where(turn == slice_index, trim_rows(padded, 6 - 2 * offset), owned)
        return (padded, owned)

    unused_state, c_points = lax.fori_loop(
        0, lax.axis_size("tm") // 4, group_fn, (initial_state, jnp.zeros_like(defect))
    )
    f_points, unused_end = advance(earlier(c_points), drag_pad, STEPS - 1, layers, False)
    return (c_points[None], f_points[None])


def solution(mesh):
    placed = (P(None, "space", None), P("tm", None, "space", None), P("space", None))
    return jax.shard_map(
        body,
        mesh=mesh,
        in_specs=placed,
        out_specs=(P("tm", None, "space", None), P("tm", None, "space", None)),
        check_vma=False,
    )
```

profile of v0, /device:TPU:0, one launch (start us, length us, event | category | flops | bytes accessed | tf_op | source)
XLA Modules:
  0.0 128.4 jit_solution(17374172756652679504)
XLA Ops:
  0.6 0.8 fusion.2103
  1.4 0.5 collective-permute-start.2
  1.9 0.8 fusion.1657
  2.6 2.7 %collective-permute-start = (f32[3,8,256]{2,1,0:T(8,128)S(1)}, f32[3,8,256]{2,1,0:T(8,128)S(1)}, u32[]{:S(2)}, u32[]{:S(2)}) collective-permute-start(f32[3,8,256]{2,1,0:T(8,128)S(1)} %get-tuple-element.361), channel_id=1, source_target_pairs={{0,1},{1,2},{2,3},{3,4},{4,5},{5,6},{6,7},{7,0},{8,9},{9,10},{10,1... | collective-permute-start | bytes 73736 | tf_op jit(solution)/shard_map/while/body/eval_jaxpr/ppermute | solution.py:21
  5.3 3.4 %collective-permute-start.4 = (f32[3,24,256]{2,1,0:T(8,128)S(1)}, f32[3,24,256]{2,1,0:T(8,128)S(1)}, u32[]{:S(2)}, u32[]{:S(2)}) collective-permute-start(f32[3,24,256]{2,1,0:T(8,128)S(1)} %bitcast.5615), channel_id=1, source_target_pairs={{0,8},{8,16},{16,24},{1,9},{9,17},{17,25},{2,10},{10,18},{18,26},{... | collective-permute-start | bytes 221192 | tf_op jit(solution)/shard_map/ppermute | solution.py:32
  8.7 1.6 %collective-permute-start.3 = (f32[8,256]{1,0:T(8,128)S(1)}, f32[8,256]{1,0:T(8,128)S(1)}, u32[]{:S(2)}, u32[]{:S(2)}) collective-permute-start(f32[8,256]{1,0:T(8,128)S(1)} %get-tuple-element.1254), channel_id=1, source_target_pairs={{1,0},{2,1},{3,2},{4,3},{5,4},{6,5},{7,6},{0,7},{9,8},{10,9},{11,1... | collective-permute-start | bytes 24584 | tf_op jit(solution)/shard_map/ppermute | solution.py:24
  10.4 0.8 collective-permute-start.1
  11.2 0.6 collective-permute-done.3
  11.7 0.3 copy-done.1
  12.0 0.6 collective-permute-done.1
  13.7 3.6 %collective-permute-start.6 = (f32[3,8,256]{2,1,0:T(8,128)S(1)}, f32[3,8,256]{2,1,0:T(8,128)S(1)}, u32[]{:S(2)}, u32[]{:S(2)}) collective-permute-start(f32[3,8,256]{2,1,0:T(8,128)S(1)} %get-tuple-element.373), channel_id=1, source_target_pairs={{1,0},{2,1},{3,2},{4,3},{5,4},{6,5},{7,6},{0,7},{9,8},{10,9},{11,1... | collective-permute-start | bytes 73736 | tf_op jit(solution)/shard_map/ppermute | solution.py:24
  17.7 1.1 collective-permute-done.6
  18.8 3.5 %collective-permute-done.5 = f32[3,8,256]{2,1,0:T(8,128)S(1)} collective-permute-done((f32[3,8,256]{2,1,0:T(8,128)S(1)}, f32[3,8,256]{2,1,0:T(8,128)S(1)}, u32[]{:S(2)}, u32[]{:S(2)}) %collective-permute-start.5) | collective-permute-done | bytes 24608 | tf_op jit(solution)/shard_map/ppermute | solution.py:21
  24.0 0.1 fusion.564
  25.1 0.1 fusion.544
  30.4 0.5 collective-permute-start.7
  30.9 0.9 collective-permute-done.8
  31.9 3.6 %collective-permute-done.7 = f32[3,8,256]{2,1,0:T(8,128)S(1)} collective-permute-done((f32[3,8,256]{2,1,0:T(8,128)S(1)}, f32[3,8,256]{2,1,0:T(8,128)S(1)}, u32[]{:S(2)}, u32[]{:S(2)}) %collective-permute-start.7) | collective-permute-done | bytes 24608 | tf_op jit(solution)/shard_map/ppermute | solution.py:21
  36.2 0.1 fusion.524
  37.3 0.1 fusion.504
  43.5 3.4 %collective-permute-start.9 = (f32[3,24,256]{2,1,0:T(8,128)S(1)}, f32[3,24,256]{2,1,0:T(8,128)S(1)}, u32[]{:S(2)}, u32[]{:S(2)}) collective-permute-start(f32[3,24,256]{2,1,0:T(8,128)S(1)} %fusion.57), channel_id=1, source_target_pairs={{0,8},{8,16},{16,24},{1,9},{9,17},{17,25},{2,10},{10,18},{18,26},{... | collective-permute-start | bytes 221192 | tf_op jit(solution)/shard_map/ppermute | solution.py:32
  46.9 0.1 fusion.604
  47.0 1.8 %collective-permute-done.9 = f32[3,24,256]{2,1,0:T(8,128)S(1)} collective-permute-done((f32[3,24,256]{2,1,0:T(8,128)S(1)}, f32[3,24,256]{2,1,0:T(8,128)S(1)}, u32[]{:S(2)}, u32[]{:S(2)}) %collective-permute-start.9) | collective-permute-done | bytes 73760 | tf_op jit(solution)/shard_map/ppermute | solution.py:32
  49.0 0.5 collective-permute-start.10
  49.5 0.9 collective-permute-done.11
  50.5 3.6 %collective-permute-done.10 = f32[3,8,256]{2,1,0:T(8,128)S(1)} collective-permute-done((f32[3,8,256]{2,1,0:T(8,128)S(1)}, f32[3,8,256]{2,1,0:T(8,128)S(1)}, u32[]{:S(2)}, u32[]{:S(2)}) %collective-permute-start.10) | collective-permute-done | bytes 24608 | tf_op jit(solution)/shard_map/ppermute | solution.py:21
  56.5 0.1 fusion.444
  62.9 0.5 collective-permute-start.12
  63.5 0.1 fusion.344
  63.7 0.7 collective-permute-done.13
  64.4 3.7 %collective-permute-done.12 = f32[3,8,256]{2,1,0:T(8,128)S(1)} collective-permute-done((f32[3,8,256]{2,1,0:T(8,128)S(1)}, f32[3,8,256]{2,1,0:T(8,128)S(1)}, u32[]{:S(2)}, u32[]{:S(2)}) %collective-permute-start.12) | collective-permute-done | bytes 24608 | tf_op jit(solution)/shard_map/ppermute | solution.py:21
  69.0 0.1 fusion.136
  70.0 0.1 fusion.384
  71.0 0.1 fusion.364
  76.3 0.5 collective-permute-start.14
  76.9 0.9 collective-permute-done.15
  77.8 3.6 %collective-permute-done.14 = f32[3,8,256]{2,1,0:T(8,128)S(1)} collective-permute-done((f32[3,8,256]{2,1,0:T(8,128)S(1)}, f32[3,8,256]{2,1,0:T(8,128)S(1)}, u32[]{:S(2)}, u32[]{:S(2)}) %collective-permute-start.14) | collective-permute-done | bytes 24608 | tf_op jit(solution)/shard_map/ppermute | solution.py:21
  81.4 11.7 %all-gather = f32[12,40,256]{2,1,0:T(8,128)S(1)} all-gather(f32[3,40,256]{2,1,0:T(8,128)S(1)} %pad_maximum_fusion.13), channel_id=2, replica_groups=mesh['tm'=4,'space'=8] {'tm'}, dimensions={0}, use_global_device_ids=true | all-gather | bytes 614400 | tf_op jit(solution)/shard_map/all_gather | solution.py:128
  99.2 2.2 %collective-permute-start.16 = (f32[3,24,256]{2,1,0:T(8,128)S(1)}, f32[3,24,256]{2,1,0:T(8,128)S(1)}, u32[]{:S(2)}, u32[]{:S(2)}) collective-permute-start(f32[3,24,256]{2,1,0:T(8,128)S(1)} %fusion.47), channel_id=1, source_target_pairs={{0,8},{8,16},{16,24},{1,9},{9,17},{17,25},{2,10},{10,18},{18,26},{... | collective-permute-start | bytes 221192 | tf_op jit(solution)/shard_map/ppermute | solution.py:32
  101.4 2.0 %collective-permute-done.16 = f32[3,24,256]{2,1,0:T(8,128)S(1)} collective-permute-done((f32[3,24,256]{2,1,0:T(8,128)S(1)}, f32[3,24,256]{2,1,0:T(8,128)S(1)}, u32[]{:S(2)}, u32[]{:S(2)}) %collective-permute-start.16) | collective-permute-done | bytes 73760 | tf_op jit(solution)/shard_map/ppermute | solution.py:32
  103.5 0.5 collective-permute-start.17
  104.0 1.0 collective-permute-done.18
  105.0 3.6 %collective-permute-done.17 = f32[3,8,256]{2,1,0:T(8,128)S(1)} collective-permute-done((f32[3,8,256]{2,1,0:T(8,128)S(1)}, f32[3,8,256]{2,1,0:T(8,128)S(1)}, u32[]{:S(2)}, u32[]{:S(2)}) %collective-permute-start.17) | collective-permute-done | bytes 24608 | tf_op jit(solution)/shard_map/ppermute | solution.py:21
  110.4 0.1 fusion.284
  116.7 0.5 collective-permute-start.19
  117.2 1.0 collective-permute-done.20
  118.2 3.6 %collective-permute-done.19 = f32[3,6,256]{2,1,0:T(8,128)S(1)} collective-permute-done((f32[3,6,256]{2,1,0:T(8,128)S(1)}, f32[3,6,256]{2,1,0:T(8,128)S(1)}, u32[]{:S(2)}, u32[]{:S(2)}) %collective-permute-start.19) | collective-permute-done | bytes 18464 | tf_op jit(solution)/shard_map/ppermute | solution.py:21
  127.7 0.7 fusion.42
  (792 shorter events, 52.3 us)
Async XLA Ops:
  0.6 4.7 %copy-start.3 = (f32[1,3,24,256]{3,2,1,0:T(8,128)S(1)}, f32[1,3,24,256]{3,2,1,0:T(8,128)}, u32[]{:S(2)}) copy-start(f32[1,3,24,256]{3,2,1,0:T(8,128)} %param.4) | copy-start | bytes 221188
  1.4 9.7 %collective-permute-start.2 = (f32[8,256]{1,0:T(8,128)S(1)}, f32[8,256]{1,0:T(8,128)S(1)}, u32[]{:S(2)}, u32[]{:S(2)}) collective-permute-start(f32[8,256]{1,0:T(8,128)S(1)} %get-tuple-element.1255), channel_id=1, source_target_pairs={{0,1},{1,2},{2,3},{3,4},{4,5},{5,6},{6,7},{7,0},{8,9},{9,10},{10,1... | collective-permute-start | bytes 24584 | tf_op jit(solution)/shard_map/ppermute | solution.py:21
  2.6 8.5 %copy-start = (f32[24,256]{1,0:T(8,128)S(1)}, f32[24,256]{1,0:T(8,128)}, u32[]{:S(2)}) copy-start(f32[24,256]{1,0:T(8,128)} %param.5) | copy-start | bytes 73732
  2.6 9.1 %collective-permute-start = (f32[3,8,256]{2,1,0:T(8,128)S(1)}, f32[3,8,256]{2,1,0:T(8,128)S(1)}, u32[]{:S(2)}, u32[]{:S(2)}) collective-permute-start(f32[3,8,256]{2,1,0:T(8,128)S(1)} %get-tuple-element.361), channel_id=1, source_target_pairs={{0,1},{1,2},{2,3},{3,4},{4,5},{5,6},{6,7},{7,0},{8,9},{9,10},{10,1... | collective-permute-start | bytes 73736 | tf_op jit(solution)/shard_map/while/body/eval_jaxpr/ppermute | solution.py:21
  5.3 6.4 %collective-permute-start.4 = (f32[3,24,256]{2,1,0:T(8,128)S(1)}, f32[3,24,256]{2,1,0:T(8,128)S(1)}, u32[]{:S(2)}, u32[]{:S(2)}) collective-permute-start(f32[3,24,256]{2,1,0:T(8,128)S(1)} %bitcast.5615), channel_id=1, source_target_pairs={{0,8},{8,16},{16,24},{1,9},{9,17},{17,25},{2,10},{10,18},{18,26},{... | collective-permute-start | bytes 221192 | tf_op jit(solution)/shard_map/ppermute | solution.py:32
  8.7 3.0 %collective-permute-start.3 = (f32[8,256]{1,0:T(8,128)S(1)}, f32[8,256]{1,0:T(8,128)S(1)}, u32[]{:S(2)}, u32[]{:S(2)}) collective-permute-start(f32[8,256]{1,0:T(8,128)S(1)} %get-tuple-element.1254), channel_id=1, source_target_pairs={{1,0},{2,1},{3,2},{4,3},{5,4},{6,5},{7,6},{0,7},{9,8},{10,9},{11,1... | collective-permute-start | bytes 24584 | tf_op jit(solution)/shard_map/ppermute | solution.py:24
  10.4 2.3 %collective-permute-start.1 = (f32[3,8,256]{2,1,0:T(8,128)S(1)}, f32[3,8,256]{2,1,0:T(8,128)S(1)}, u32[]{:S(2)}, u32[]{:S(2)}) collective-permute-start(f32[3,8,256]{2,1,0:T(8,128)S(1)} %get-tuple-element.360), channel_id=1, source_target_pairs={{1,0},{2,1},{3,2},{4,3},{5,4},{6,5},{7,6},{0,7},{9,8},{10,9},{11,1... | collective-permute-start | bytes 73736 | tf_op jit(solution)/shard_map/while/body/eval_jaxpr/ppermute | solution.py:24
  11.1 0.9 copy-start.1
  13.7 5.1 %collective-permute-start.6 = (f32[3,8,256]{2,1,0:T(8,128)S(1)}, f32[3,8,256]{2,1,0:T(8,128)S(1)}, u32[]{:S(2)}, u32[]{:S(2)}) collective-permute-start(f32[3,8,256]{2,1,0:T(8,128)S(1)} %get-tuple-element.373), channel_id=1, source_target_pairs={{1,0},{2,1},{3,2},{4,3},{5,4},{6,5},{7,6},{0,7},{9,8},{10,9},{11,1... | collective-permute-start | bytes 73736 | tf_op jit(solution)/shard_map/ppermute | solution.py:24
  17.3 5.0 %collective-permute-start.5 = (f32[3,8,256]{2,1,0:T(8,128)S(1)}, f32[3,8,256]{2,1,0:T(8,128)S(1)}, u32[]{:S(2)}, u32[]{:S(2)}) collective-permute-start(f32[3,8,256]{2,1,0:T(8,128)S(1)} %get-tuple-element.372), channel_id=1, source_target_pairs={{0,1},{1,2},{2,3},{3,4},{4,5},{5,6},{6,7},{7,0},{8,9},{9,10},{10,1... | collective-permute-start | bytes 73736 | tf_op jit(solution)/shard_map/ppermute | solution.py:21
  30.3 1.6 %collective-permute-start.8 = (f32[3,8,256]{2,1,0:T(8,128)S(1)}, f32[3,8,256]{2,1,0:T(8,128)S(1)}, u32[]{:S(2)}, u32[]{:S(2)}) collective-permute-start(f32[3,8,256]{2,1,0:T(8,128)S(1)} %get-tuple-element.371), channel_id=1, source_target_pairs={{1,0},{2,1},{3,2},{4,3},{5,4},{6,5},{7,6},{0,7},{9,8},{10,9},{11,1... | collective-permute-start | bytes 73736 | tf_op jit(solution)/shard_map/ppermute | solution.py:24
  30.4 5.1 %collective-permute-start.7 = (f32[3,8,256]{2,1,0:T(8,128)S(1)}, f32[3,8,256]{2,1,0:T(8,128)S(1)}, u32[]{:S(2)}, u32[]{:S(2)}) collective-permute-start(f32[3,8,256]{2,1,0:T(8,128)S(1)} %get-tuple-element.370), channel_id=1, source_target_pairs={{0,1},{1,2},{2,3},{3,4},{4,5},{5,6},{6,7},{7,0},{8,9},{9,10},{10,1... | collective-permute-start | bytes 73736 | tf_op jit(solution)/shard_map/ppermute | solution.py:21
  43.5 5.4 %collective-permute-start.9 = (f32[3,24,256]{2,1,0:T(8,128)S(1)}, f32[3,24,256]{2,1,0:T(8,128)S(1)}, u32[]{:S(2)}, u32[]{:S(2)}) collective-permute-start(f32[3,24,256]{2,1,0:T(8,128)S(1)} %fusion.57), channel_id=1, source_target_pairs={{0,8},{8,16},{16,24},{1,9},{9,17},{17,25},{2,10},{10,18},{18,26},{... | collective-permute-start | bytes 221192 | tf_op jit(solution)/shard_map/ppermute | solution.py:32
  48.9 1.6 %collective-permute-start.11 = (f32[3,8,256]{2,1,0:T(8,128)S(1)}, f32[3,8,256]{2,1,0:T(8,128)S(1)}, u32[]{:S(2)}, u32[]{:S(2)}) collective-permute-start(f32[3,8,256]{2,1,0:T(8,128)S(1)} %get-tuple-element.369), channel_id=1, source_target_pairs={{1,0},{2,1},{3,2},{4,3},{5,4},{6,5},{7,6},{0,7},{9,8},{10,9},{11,1... | collective-permute-start | bytes 73736 | tf_op jit(solution)/shard_map/ppermute | solution.py:24
  49.0 5.1 %collective-permute-start.10 = (f32[3,8,256]{2,1,0:T(8,128)S(1)}, f32[3,8,256]{2,1,0:T(8,128)S(1)}, u32[]{:S(2)}, u32[]{:S(2)}) collective-permute-start(f32[3,8,256]{2,1,0:T(8,128)S(1)} %get-tuple-element.368), channel_id=1, source_target_pairs={{0,1},{1,2},{2,3},{3,4},{4,5},{5,6},{6,7},{7,0},{8,9},{9,10},{10,1... | collective-permute-start | bytes 73736 | tf_op jit(solution)/shard_map/ppermute | solution.py:21
  62.8 1.6 %collective-permute-start.13 = (f32[3,8,256]{2,1,0:T(8,128)S(1)}, f32[3,8,256]{2,1,0:T(8,128)S(1)}, u32[]{:S(2)}, u32[]{:S(2)}) collective-permute-start(f32[3,8,256]{2,1,0:T(8,128)S(1)} %get-tuple-element.367), channel_id=1, source_target_pairs={{1,0},{2,1},{3,2},{4,3},{5,4},{6,5},{7,6},{0,7},{9,8},{10,9},{11,1... | collective-permute-start | bytes 73736 | tf_op jit(solution)/shard_map/ppermute | solution.py:24
  62.9 5.3 %collective-permute-start.12 = (f32[3,8,256]{2,1,0:T(8,128)S(1)}, f32[3,8,256]{2,1,0:T(8,128)S(1)}, u32[]{:S(2)}, u32[]{:S(2)}) collective-permute-start(f32[3,8,256]{2,1,0:T(8,128)S(1)} %get-tuple-element.366), channel_id=1, source_target_pairs={{0,1},{1,2},{2,3},{3,4},{4,5},{5,6},{6,7},{7,0},{8,9},{9,10},{10,1... | collective-permute-start | bytes 73736 | tf_op jit(solution)/shard_map/ppermute | solution.py:21
  76.2 1.6 %collective-permute-start.15 = (f32[3,8,256]{2,1,0:T(8,128)S(1)}, f32[3,8,256]{2,1,0:T(8,128)S(1)}, u32[]{:S(2)}, u32[]{:S(2)}) collective-permute-start(f32[3,8,256]{2,1,0:T(8,128)S(1)} %get-tuple-element.365), channel_id=1, source_target_pairs={{1,0},{2,1},{3,2},{4,3},{5,4},{6,5},{7,6},{0,7},{9,8},{10,9},{11,1... | collective-permute-start | bytes 73736 | tf_op jit(solution)/shard_map/ppermute | solution.py:24
  76.3 5.1 %collective-permute-start.14 = (f32[3,8,256]{2,1,0:T(8,128)S(1)}, f32[3,8,256]{2,1,0:T(8,128)S(1)}, u32[]{:S(2)}, u32[]{:S(2)}) collective-permute-start(f32[3,8,256]{2,1,0:T(8,128)S(1)} %get-tuple-element.364), channel_id=1, source_target_pairs={{0,1},{1,2},{2,3},{3,4},{4,5},{5,6},{6,7},{7,0},{8,9},{9,10},{10,1... | collective-permute-start | bytes 73736 | tf_op jit(solution)/shard_map/ppermute | solution.py:21
  99.2 4.2 %copy-start.2 = (f32[3,24,256]{2,1,0:T(8,128)}, f32[3,24,256]{2,1,0:T(8,128)S(1)}, u32[]{:S(2)}) copy-start(f32[3,24,256]{2,1,0:T(8,128)S(1)} %fusion.47) | copy-start | bytes 221188
  99.2 4.2 %collective-permute-start.16 = (f32[3,24,256]{2,1,0:T(8,128)S(1)}, f32[3,24,256]{2,1,0:T(8,128)S(1)}, u32[]{:S(2)}, u32[]{:S(2)}) collective-permute-start(f32[3,24,256]{2,1,0:T(8,128)S(1)} %fusion.47), channel_id=1, source_target_pairs={{0,8},{8,16},{16,24},{1,9},{9,17},{17,25},{2,10},{10,18},{18,26},{... | collective-permute-start | bytes 221192 | tf_op jit(solution)/shard_map/ppermute | solution.py:32
  103.4 1.6 %collective-permute-start.18 = (f32[3,8,256]{2,1,0:T(8,128)S(1)}, f32[3,8,256]{2,1,0:T(8,128)S(1)}, u32[]{:S(2)}, u32[]{:S(2)}) collective-permute-start(f32[3,8,256]{2,1,0:T(8,128)S(1)} %get-tuple-element.359), channel_id=1, source_target_pairs={{1,0},{2,1},{3,2},{4,3},{5,4},{6,5},{7,6},{0,7},{9,8},{10,9},{11,1... | collective-permute-start | bytes 73736 | tf_op jit(solution)/shard_map/ppermute | solution.py:24
  103.5 5.1 %collective-permute-start.17 = (f32[3,8,256]{2,1,0:T(8,128)S(1)}, f32[3,8,256]{2,1,0:T(8,128)S(1)}, u32[]{:S(2)}, u32[]{:S(2)}) collective-permute-start(f32[3,8,256]{2,1,0:T(8,128)S(1)} %get-tuple-element.358), channel_id=1, source_target_pairs={{0,1},{1,2},{2,3},{3,4},{4,5},{5,6},{6,7},{7,0},{8,9},{9,10},{10,1... | collective-permute-start | bytes 73736 | tf_op jit(solution)/shard_map/ppermute | solution.py:21
  116.6 1.6 %collective-permute-start.20 = (f32[3,6,256]{2,1,0:T(8,128)S(1)}, f32[3,6,256]{2,1,0:T(8,128)S(1)}, u32[]{:S(2)}, u32[]{:S(2)}) collective-permute-start(f32[3,6,256]{2,1,0:T(8,128)S(1)} %get-tuple-element.357), channel_id=1, source_target_pairs={{1,0},{2,1},{3,2},{4,3},{5,4},{6,5},{7,6},{0,7},{9,8},{10,9},{11,1... | collective-permute-start | bytes 55304 | tf_op jit(solution)/shard_map/ppermute | solution.py:24
  116.7 5.1 %collective-permute-start.19 = (f32[3,6,256]{2,1,0:T(8,128)S(1)}, f32[3,6,256]{2,1,0:T(8,128)S(1)}, u32[]{:S(2)}, u32[]{:S(2)}) collective-permute-start(f32[3,6,256]{2,1,0:T(8,128)S(1)} %get-tuple-element.356), channel_id=1, source_target_pairs={{0,1},{1,2},{2,3},{3,4},{4,5},{5,6},{6,7},{7,0},{8,9},{9,10},{10,1... | collective-permute-start | bytes 55304 | tf_op jit(solution)/shard_map/ppermute | solution.py:21
where the time goes:
time: 129 us; the launch traced here: 128 us
  waiting for transfers between devices  36.8 us (29%)
  local copies, waits for them, and re-layouts  34.8 us (27%)
  starting transfers between devices  21.5 us (17%)
  other arithmetic  20.8 us (16%)
  blocking collectives  11.7 us (9%)
  between operations  2.78 us (2%)
    ppermute x9, waiting for transfers between devices, with_halo(): lax.ppermute(lax.slice_in_dim(block, block.shape[dim] - width, None, axis...  25.2 us
    slice x326, local copies, waits for them, and re-layouts, cut_neighbours(): jnp.roll(field, 1, 1)[1:-1]  24.3 us
    another operation x165, other arithmetic, tendency(): return jnp.stack([rate_height, rate_row, rate_col])  17.3 us
    all_gather x1, blocking collectives, body(): gathered = lax.all_gather(defect_pad[None], 'tm', axis=0, tiled=True)  11.7 us
    ppermute x3, starting transfers between devices, shifted(): return lax.ppermute(value, axis, pairs)  8.98 us
    slice x110, local copies, waits for them, and re-layouts, cut_neighbours(): jnp.roll(field, -1, 1)[1:-1]  8.11 us
    ppermute x9, waiting for transfers between devices, with_halo(): lax.ppermute(lax.slice_in_dim(block, 0, width, axis=dim), axis, backward)  7.84 us
    ppermute x9, starting transfers between devices, with_halo(): lax.ppermute(lax.slice_in_dim(block, 0, width, axis=dim), axis, backward)  6.38 us
  transfers between devices with their start and end apart: 21, of which 18 were waited for; matrix products, arithmetic and copies ran while one was open for 1% of the time, Pallas kernels for 0%

commit v1 on v0

v1 whole, which is shorter than its diff:
```python
import jax
import jax.numpy as jnp
from jax import lax
from jax.experimental import pallas as pl
from jax.experimental.pallas import tpu as pltpu
from jax.sharding import PartitionSpec as P

STEPS = 8


gravity = 2.0
coriolis = 0.5
viscosity = 0.5
time_step = 0.04

LANES = 128
BLOCK = 8
VMEM = pl.BlockSpec(memory_space=pltpu.VMEM)
SMEM = pl.BlockSpec(memory_space=pltpu.SMEM)


def across(tiles):
    count = len(tiles)
    lane = lax.broadcasted_iota(jnp.int32, tiles[0].shape, 1)
    up = [pltpu.roll(tile, LANES - 1, 1) for tile in tiles]
    down = [pltpu.roll(tile, 1, 1) for tile in tiles]
    east = [jnp.where(lane == LANES - 1, up[(i + 1) % count], up[i]) for i in range(count)]
    west = [jnp.where(lane == 0, down[i - 1], down[i]) for i in range(count)]
    return east, west


def slopes(src, row, tiles):
    here = [[src[f, i, pl.ds(row, BLOCK), :] for i in range(tiles)] for f in range(3)]
    north = [[src[f, i, pl.ds(row + 1, BLOCK), :] for i in range(tiles)] for f in range(3)]
    south = [[src[f, i, pl.ds(row - 1, BLOCK), :] for i in range(tiles)] for f in range(3)]
    sides = [across(here[f]) for f in range(3)]
    out = []
    for i in range(tiles):
        u, w = here[1][i], here[2][i]
        en, un, wn = (north[f][i] for f in range(3))
        es, us, ws = (south[f][i] for f in range(3))
        ee, ue, we = (sides[f][0][i] for f in range(3))
        ew, uw, ww = (sides[f][1][i] for f in range(3))
        un_us, we_ww = un - us, we - ww
        rest_e = (en * (1.0 - un) + es * (1.0 + us)) + (ee * (1.0 - we) + ew * (1.0 + ww))
        rest_e = (rest_e - un_us) - we_ww
        rest_u = ((un + us) - u * un_us) + ((ue + uw) - w * (ue - uw))
        rest_w = ((wn + ws) - u * (wn - ws)) + ((we + ww) - w * we_ww)
        rest_u = rest_u + ((2.0 * coriolis) * w - (2.0 * gravity * 0.5) * (en - es))
        rest_w = rest_w - ((2.0 * coriolis) * u + (2.0 * gravity * 0.5) * (ee - ew))
        out.append((rest_e, rest_u, rest_w))
    return here, out


def own_factor(keep, i, row, size):
    kept = keep[i, pl.ds(row, BLOCK), :]
    ratio = size / time_step
    return kept if ratio == 1.0 else ratio * kept + (1.0 - ratio)


def first_stage(src, mid, keep, blocks, pad, size, tiles):
    for block in blocks:
        row = pad + BLOCK * block
        here, rest = slopes(src, row, tiles)
        for i in range(tiles):
            factor = own_factor(keep, i, row, size)
            for f in range(3):
                own = (1.0 - 2.0 * size) if f == 0 else factor
                mid[f, i, pl.ds(row, BLOCK), :] = own * here[f][i] + (0.5 * size) * rest[i][f]


def second_stage(src, mid, keep, blocks, pad, size, tiles, put):
    for block in blocks:
        row = pad + BLOCK * block
        here, rest = slopes(mid, row, tiles)
        for i in range(tiles):
            factor = own_factor(keep, i, row, size)
            for f in range(3):
                own = (1.0 - 2.0 * size) if f == 0 else factor
                old = src[f, i, pl.ds(row, BLOCK), :]
                new = 0.5 * ((old + own * here[f][i]) + (0.5 * size) * rest[i][f])
                put(block, f, i, old, new)


def fine_kernel(layout, which_ref, *refs):
    count, strip, margin, tiles, slices = layout
    parts = refs[: 2 * count + 1]
    narrow_ref, far_ref, wide_ref, state, mid, keep, before, coarse = refs[2 * count + 1 :]
    rows = (2 * count + 1) * strip
    pad = BLOCK
    centre = count * strip // BLOCK
    strip_blocks = range(centre, centre + strip // BLOCK)
    total = rows // BLOCK
    reach = 4 * STEPS
    which = which_ref[0]

    for ref in (state, mid):
        for f in range(3):
            for i in range(tiles):
                for row in (0, pad + rows):
                    ref[f, i, pl.ds(row, BLOCK), :] = jnp.zeros((BLOCK, LANES), jnp.float32)
    for p, part in enumerate(parts):
        for b in range(strip // BLOCK):
            row = pad + p * strip + b * BLOCK
            for i in range(tiles):
                columns = pl.ds(i * LANES, LANES)
                for f in range(3):
                    state[f, i, pl.ds(row, BLOCK), :] = part[f, pl.ds(b * BLOCK, BLOCK), columns]
                drag = part[3, pl.ds(b * BLOCK, BLOCK), columns]
                keep[i, pl.ds(row, BLOCK), :] = (1.0 - 2.0 * time_step) - time_step * drag

    def put(block, f, i, old, new):
        if block in strip_blocks:
            before[f, i, pl.ds((block - centre) * BLOCK, BLOCK), :] = old
        state[f, i, pl.ds(pad + BLOCK * block, BLOCK), :] = new

    def steps(start, group):
        first, last = start // BLOCK, total - start // BLOCK

        def one(turn, carry):
            first_stage(state, mid, keep, range(first, last), pad, time_step, tiles)
            second_stage(state, mid, keep, range(first, last), pad, time_step, tiles, put)
            return carry

        lax.fori_loop(0, group, one, 0)

    def emit(target, source, rows_from, row_count):
        for f in range(3):
            for i in range(tiles):
                for b in range(0, row_count, BLOCK):
                    take = min(BLOCK, row_count - b)
                    target[f, pl.ds(b, take), pl.ds(i * LANES, LANES)] = source(f, i, rows_from + b, take)

    def from_state(f, i, row, take):
        return state[f, i, pl.ds(pad + row, take), :]

    def from_before(f, i, row, take):
        return before[f, i, pl.ds(row, take), :]

    group = BLOCK // 2
    for start in range(0, STEPS, group):
        steps(2 * start, group)

    edge = count * strip - margin
    out_first, out_last = edge // BLOCK, (edge + strip + 2 * margin) // BLOCK

    @pl.when(which == slices - 2)
    def _():
        emit(narrow_ref, from_state, count * strip, strip)
        emit(far_ref, from_before, 0, strip)

    def put_coarse(block, f, i, old, new):
        coarse[f, i, pl.ds((block - out_first) * BLOCK, BLOCK), :] = new

    size = STEPS * time_step
    first_stage(state, mid, keep, range(out_first - 1, out_last + 1), pad, size, tiles)
    second_stage(state, mid, keep, range(out_first, out_last), pad, size, tiles, put_coarse)

    for start in range(STEPS, 2 * STEPS, group):
        steps(2 * start, group)

    def from_defect(f, i, row, take):
        return state[f, i, pl.ds(pad + row, take), :] - coarse[f, i, pl.ds(row - edge, take), :]

    wide = strip + 2 * margin

    @pl.when(which < slices - 2)
    def _():
        emit(narrow_ref, from_defect, count * strip, strip)
        emit(far_ref, from_defect, edge + 2, wide - 4)
        emit(wide_ref, from_defect, edge, wide)

    @pl.when(which >= slices - 2)
    def _():
        emit(wide_ref, from_state, edge, wide)

    @pl.when(which == slices - 1)
    def _():
        emit(narrow_ref, from_state, count * strip, strip)
        emit(far_ref, from_before, 0, strip)


def fine_chain(which, parts, margin, slices):
    count = len(parts) // 2
    strip, columns = parts[0].shape[1:]
    tiles = columns // LANES
    wide = strip + 2 * margin
    rows = len(parts) * strip + 2 * BLOCK
    shape = lambda n: jax.ShapeDtypeStruct((3, n, columns), jnp.float32)
    layout = (count, strip, margin, tiles, slices)
    return pl.pallas_call(
        lambda *refs: fine_kernel(layout, *refs),
        name="fine_chain",
        out_shape=(shape(strip), shape(wide - 4), shape(wide)),
        in_specs=[SMEM] + [VMEM] * len(parts),
        out_specs=(VMEM, VMEM, VMEM),
        scratch_shapes=[
            pltpu.VMEM((3, tiles, rows, LANES), jnp.float32),
            pltpu.VMEM((3, tiles, rows, LANES), jnp.float32),
            pltpu.VMEM((tiles, rows, LANES), jnp.float32),
            pltpu.VMEM((3, tiles, strip, LANES), jnp.float32),
            pltpu.VMEM((3, tiles, wide, LANES), jnp.float32),
        ],
    )(which, *parts)


def last_kernel(layout, which_ref, wide_ref, defects_ref, narrow_ref, far_ref, *refs):
    strip, margin, tiles, drag_from, count = layout
    drags = refs[:count]
    c_ref, f_ref, state, mid, keep = refs[count:]
    wide = strip + 2 * margin
    pad = BLOCK
    which = which_ref[0]
    total = wide // BLOCK
    chain = defects_ref.shape[0]

    for ref in (state, mid):
        for f in range(3):
            for i in range(tiles):
                for row in (0, pad + wide):
                    ref[f, i, pl.ds(row, BLOCK), :] = jnp.zeros((BLOCK, LANES), jnp.float32)
    for b in range(total):
        at = drag_from + b * BLOCK
        part = drags[at // strip]
        for i in range(tiles):
            columns = pl.ds(i * LANES, LANES)
            drag = part[3, pl.ds(at % strip, BLOCK), columns]
            keep[i, pl.ds(pad + b * BLOCK, BLOCK), :] = (1.0 - 2.0 * time_step) - time_step * drag
            for f in range(3):
                state[f, i, pl.ds(pad + b * BLOCK, BLOCK), :] = wide_ref[f, pl.ds(b * BLOCK, BLOCK), columns]

    coarse_size = STEPS * time_step

    def put(block, f, i, old, new):
        state[f, i, pl.ds(pad + BLOCK * block, BLOCK), :] = new

    def link(turn):
        first_stage(state, mid, keep, range(total), pad, coarse_size, tiles)
        second_stage(state, mid, keep, range(total), pad, coarse_size, tiles, put)
        for f in range(3):
            for i in range(tiles):
                for b in range(0, wide - 4, BLOCK):
                    take = min(BLOCK, wide - 4 - b)
                    add = defects_ref[turn, f, pl.ds(b, take), pl.ds(i * LANES, LANES)]
                    at = pl.ds(pad + 2 + b, take)
                    state[f, i, at, :] = state[f, i, at, :] + add

    for turn in range(chain):
        pl.when(which > turn + 2)(lambda: link(turn))

    first = margin // BLOCK
    strip_blocks = range(first, first + strip // BLOCK)

    def put_c(block, f, i, old, new):
        b = (block - first) * BLOCK
        columns = pl.ds(i * LANES, LANES)
        value = narrow_ref[f, pl.ds(b, BLOCK), columns]
        c_ref[f, pl.ds(b, BLOCK), columns] = jnp.where(which < 2, value, new + value)

    def put_f(block, f, i, old, new):
        b = (block - first) * BLOCK
        columns = pl.ds(i * LANES, LANES)
        value = far_ref[f, pl.ds(b, BLOCK), columns]
        f_ref[f, pl.ds(b, BLOCK), columns] = jnp.where(which < 2, value, new)

    first_stage(state, mid, keep, range(first - 1, first + strip // BLOCK + 1), pad, coarse_size, tiles)
    second_stage(state, mid, keep, strip_blocks, pad, coarse_size, tiles, put_c)

    def one(turn, carry):
        first_stage(state, mid, keep, range(total), pad, time_step, tiles)
        second_stage(state, mid, keep, range(total), pad, time_step, tiles, put)
        return carry

    lax.fori_loop(0, STEPS - 2, one, 0)
    first_stage(state, mid, keep, range(first - 1, first + strip // BLOCK + 1), pad, time_step, tiles)
    second_stage(state, mid, keep, strip_blocks, pad, time_step, tiles, put_f)


def last_chain(which, wide, defects, narrow, far, parts, margin):
    strip, columns = narrow.shape[1:]
    tiles = columns // LANES
    rows = strip + 2 * margin + 2 * BLOCK
    count = len(parts)
    layout = (strip, margin, tiles, (count // 2) * strip - margin, count)
    shape = jax.ShapeDtypeStruct((3, strip, columns), jnp.float32)
    return pl.pallas_call(
        lambda *refs: last_kernel(layout, *refs),
        name="last_chain",
        out_shape=(shape, shape),
        in_specs=[SMEM] + [VMEM] * (4 + count),
        out_specs=(VMEM, VMEM),
        scratch_shapes=[
            pltpu.VMEM((3, tiles, rows, LANES), jnp.float32),
            pltpu.VMEM((3, tiles, rows, LANES), jnp.float32),
            pltpu.VMEM((tiles, rows, LANES), jnp.float32),
        ],
    )(which, wide, defects, narrow, far, *parts)


def body(initial_state, c_guess, friction):
    slices, strips = lax.axis_size("tm"), lax.axis_size("space")
    strip = initial_state.shape[1]
    which = lax.axis_index("tm")
    margin = 2 * (STEPS - 1) + 2 * (slices - 3)
    count = -(-(4 * STEPS + margin) // strip)
    both = ("tm", "space")

    def moved(value, target):
        pairs = []
        for t in range(slices):
            for s in range(strips):
                to = target(t, s)
                if to is not None:
                    pairs.append((t * strips + s, to[0] * strips + to[1] % strips))
        return lax.ppermute(value, both, pairs)

    start = jnp.where(which >= slices - 2, initial_state, c_guess[0])
    own = jnp.concatenate([start, friction[None]], axis=0)
    parts = []
    for offset in range(-count, count + 1):
        parts.append(own if offset == 0 else moved(own, lambda t, s, o=offset: (t, s - o)))
    index = which.astype(jnp.int32).reshape(1)
    narrow, far, wide = fine_chain(index, parts, margin, slices)

    got = moved(narrow, lambda t, s: ((t + 2) % slices, s))
    lasts = {slices - 2: 0, slices - 1: 1}
    if slices == 4:
        lasts[0] = slices - 1
    got_far = moved(far, lambda t, s: (lasts[t], s) if t in lasts else None)
    if slices == 4:
        defects = got_far[None]
    else:
        everyone = lax.all_gather(wide, "tm", axis=0)
        defects = everyone[: slices - 3, :, 2:-2]
        wide = everyone[slices - 1]
    c_points, f_points = last_chain(index, wide, defects, got, got_far, parts, margin)
    return (c_points[None], f_points[None])


def solution(mesh):
    placed = (P(None, "space", None), P("tm", None, "space", None), P("space", None))
    return jax.shard_map(
        body,
        mesh=mesh,
        in_specs=placed,
        out_specs=(P("tm", None, "space", None), P("tm", None, "space", None)),
        check_vma=False,
    )
```

time: 129 us -> 39.4 us (0.31)
  local copies, waits for them, and re-layouts: 34.8 us -> 1.32 us
  waiting for transfers between devices: 36.8 us -> 12.3 us
  other arithmetic: 20.8 us -> 0.91 us
  Pallas kernels: 0 us -> 13.1 us
  blocking collectives: 11.7 us -> 0 us
  starting transfers between devices: 21.5 us -> 10.7 us
  between operations: 2.78 us -> 0.71 us
    slice x445 -> x0, local copies, waits for them, and re-layouts: 34 us -> none  [the longest x326 24.3 us: cut_neighbours(): jnp.roll(field, 1, 1)[1:-1]]
    ppermute x21 -> x6, waiting for transfers between devices: 36.8 us -> 12.3 us  [moved(): return lax.ppermute(value, both, pairs)]
    another operation x165 -> x0, other arithmetic: 17.3 us -> none  [tendency(): return jnp.stack([rate_height, rate_row, rate_col])]
    pallas_call x0 -> x2, Pallas kernels: none -> 13.1 us  [the longest x1 9.04 us: fine_chain(): pl.pallas_call(lambda *refs: fine_kernel(layout, *refs), name='fine_chain...]
    all_gather x1 -> x0, blocking collectives: 11.7 us -> none  [body(): gathered = lax.all_gather(defect_pad[None], 'tm', axis=0, tiled=True)]
    ppermute x21 -> x6, starting transfers between devices: 21.5 us -> 10.7 us  [moved(): return lax.ppermute(value, both, pairs)]
    add x51 -> x0, other arithmetic: 1.63 us -> none  [the longest x21 0.76 us: heun_step(): return fields[:, 2:-2] + 0.5 * size * (slope_one[:, 1:-1] + slope_two)]
  transfers between devices with their start and end apart: 21 -> 6, of which waited for: 18 -> 5; matrix products, arithmetic and copies ran while one was open for 1% -> 0% of each run, Pallas kernels for 0% -> 0%
where the time goes in v1:
time: 39.4 us; the launch traced here: 39.2 us
  Pallas kernels  13.1 us (33%)
  waiting for transfers between devices  12.3 us (31%)
  starting transfers between devices  10.7 us (27%)
  local copies, waits for them, and re-layouts  1.32 us (3%)
  other arithmetic  0.91 us (2%)
  between operations  0.71 us (2%)
    ppermute x6, waiting for transfers between devices, moved(): return lax.ppermute(value, both, pairs)  12.3 us
    ppermute x6, starting transfers between devices, moved(): return lax.ppermute(value, both, pairs)  10.7 us
    pallas_call x1, Pallas kernels, fine_chain(): pl.pallas_call(lambda *refs: fine_kernel(layout, *refs), name='fine_chain...  9.04 us
    pallas_call x1, Pallas kernels, last_chain(): pl.pallas_call(lambda *refs: last_kernel(layout, *refs), name='last_chain...  4.09 us
    unnamed x16, local copies, waits for them, and re-layouts  1.32 us
    select_n x1, other arithmetic, body(): start = jnp.where(which >= slices - 2, initial_state, c_guess[0])  0.9 us
  transfers between devices with their start and end apart: 6, of which 5 were waited for; matrix products, arithmetic and copies ran while one was open for 0% of the time, Pallas kernels for 0%

profile of v1, /device:TPU:0, one launch (start us, length us, event | category | flops | bytes accessed | tf_op | source)
XLA Modules:
  0.0 39.2 jit_solution(244250351235820754)
XLA Ops:
  0.6 0.0 copy-start.7
  0.6 0.9 %bitcast_select_fusion = f32[3,24,256]{2,1,0:T(8,128)S(1)} fusion(f32[3,24,256]{2,1,0:T(8,128)} %param.3, f32[1,3,24,256]{3,2,1,0:T(8,128)} %param.4, pred[]{:T(512)S(6)} %ge.3), kind=kLoop, calls=%fused_computation.1 | loop fusion | flops 18432 | bytes 221185 | tf_op jit(solution)/shard_map/jit(_where)/select_n | solution.py:317
  1.6 0.0 copy-done.7
  1.6 0.0 copy-start
  1.6 5.1 %collective-permute-start.3 = (f32[4,24,256]{2,1,0:T(8,128)S(1)}, f32[4,24,256]{2,1,0:T(8,128)S(1)}, u32[]{:S(2)}, u32[]{:S(2)}) collective-permute-start(f32[4,24,256]{2,1,0:T(8,128)S(1)} %pad_maximum_fusion.refs_3_.refs_7_), channel_id=1, source_target_pairs={{0,6},{1,7},{2,0},{3,1},{4,2},{5,3},{6,4},{7,5},{8,14},{9,15},{10,... | collective-permute-start | bytes 294920 | tf_op jit(solution)/shard_map/ppermute | solution.py:315
  6.7 0.0 collective-permute-start.2
  6.7 0.5 %collective-permute-start.1 = (f32[4,24,256]{2,1,0:T(8,128)S(1)}, f32[4,24,256]{2,1,0:T(8,128)S(1)}, u32[]{:S(2)}, u32[]{:S(2)}) collective-permute-start(f32[4,24,256]{2,1,0:T(8,128)S(1)} %pad_maximum_fusion.refs_3_.refs_7_), channel_id=1, source_target_pairs={{0,1},{1,2},{2,3},{3,4},{4,5},{5,6},{6,7},{7,0},{8,9},{9,10},{10,1... | collective-permute-start | bytes 294920 | tf_op jit(solution)/shard_map/ppermute | solution.py:315
  7.2 0.7 %collective-permute-start = (f32[4,24,256]{2,1,0:T(8,128)S(1)}, f32[4,24,256]{2,1,0:T(8,128)S(1)}, u32[]{:S(2)}, u32[]{:S(2)}) collective-permute-start(f32[4,24,256]{2,1,0:T(8,128)S(1)} %pad_maximum_fusion.refs_3_.refs_7_), channel_id=1, source_target_pairs={{0,2},{1,3},{2,4},{3,5},{4,6},{5,7},{6,0},{7,1},{8,10},{9,11},{10,... | collective-permute-start | bytes 294920 | tf_op jit(solution)/shard_map/ppermute | solution.py:315
  7.9 1.4 %collective-permute-done.3.refs_5_.refs_9_ = f32[4,24,256]{2,1,0:T(8,128)S(1)} collective-permute-done((f32[4,24,256]{2,1,0:T(8,128)S(1)}, f32[4,24,256]{2,1,0:T(8,128)S(1)}, u32[]{:S(2)}, u32[]{:S(2)}) %collective-permute-start.3) | collective-permute-done | bytes 98336 | tf_op jit(solution)/shard_map/ppermute | solution.py:315
  9.3 0.0 copy-start.2
  9.3 2.1 %collective-permute-done.2.refs_4_.refs_8_ = f32[4,24,256]{2,1,0:T(8,128)S(1)} collective-permute-done((f32[4,24,256]{2,1,0:T(8,128)S(1)}, f32[4,24,256]{2,1,0:T(8,128)S(1)}, u32[]{:S(2)}, u32[]{:S(2)}) %collective-permute-start.2) | collective-permute-done | bytes 98336 | tf_op jit(solution)/shard_map/ppermute | solution.py:315
  11.4 0.0 copy-start.3
  11.4 1.2 %collective-permute-done.1.refs_2_.refs_6_ = f32[4,24,256]{2,1,0:T(8,128)S(1)} collective-permute-done((f32[4,24,256]{2,1,0:T(8,128)S(1)}, f32[4,24,256]{2,1,0:T(8,128)S(1)}, u32[]{:S(2)}, u32[]{:S(2)}) %collective-permute-start.1) | collective-permute-done | bytes 98336 | tf_op jit(solution)/shard_map/ppermute | solution.py:315
  12.6 0.0 copy-start.4
  12.6 2.1 %collective-permute-done.refs_1_.refs_5_ = f32[4,24,256]{2,1,0:T(8,128)S(1)} collective-permute-done((f32[4,24,256]{2,1,0:T(8,128)S(1)}, f32[4,24,256]{2,1,0:T(8,128)S(1)}, u32[]{:S(2)}, u32[]{:S(2)}) %collective-permute-start) | collective-permute-done | bytes 98336 | tf_op jit(solution)/shard_map/ppermute | solution.py:315
  14.7 0.0 copy-start.5
  14.7 0.0 copy-done
  14.7 0.0 copy-done.2
  14.7 0.0 copy-done.3
  14.7 0.0 copy-done.4
  14.7 0.6 %copy-done.5 = f32[4,24,256]{2,1,0:T(8,128)} copy-done((f32[4,24,256]{2,1,0:T(8,128)}, f32[4,24,256]{2,1,0:T(8,128)S(1)}, u32[]{:S(2)}) %copy-start.5) | copy-done | bytes 98328
  15.3 9.0 %fine_chain.1 = (f32[3,24,256]{2,1,0:T(8,128)}, f32[3,52,256]{2,1,0:T(8,128)}, f32[3,56,256]{2,1,0:T(8,128)}) custom-call(s32[1]{0:T(128)} %bitcast.refs_0_, f32[4,24,256]{2,1,0:T(8,128)} %copy-done.5, f32[4,24,256]{2,1,0:T(8,128)} %copy-done.4, f32[4,24,256]{2,1,0:T(8,128)} %copy-done, f32[4,24,256]{2,1,0:T(8,128)} %copy-done.3, f32[4,24,256]{2,1,0:T(8,128)} %copy-done.2), custom_call_target="tpu_custom_call" | custom-call | tf_op jit(solution)/shard_map/fine_chain/pallas_call | solution.py:191
  24.3 4.4 %collective-permute-start.4 = (f32[3,52,256]{2,1,0:T(8,128)}, f32[3,52,256]{2,1,0:T(8,128)S(1)}, u32[]{:S(2)}, u32[]{:S(2)}) collective-permute-start(f32[3,52,256]{2,1,0:T(8,128)} %get-tuple-element.8), channel_id=1, source_target_pairs={{0,24},{1,25},{2,26},{3,27},{4,28},{5,29},{6,30},{7,31},{16,0},{17... | collective-permute-start | bytes 479240 | tf_op jit(solution)/shard_map/ppermute | solution.py:315
  28.7 0.1 collective-permute-start.5
  28.8 5.6 %collective-permute-done.5.refs_3_ = f32[3,24,256]{2,1,0:T(8,128)S(1)} collective-permute-done((f32[3,24,256]{2,1,0:T(8,128)}, f32[3,24,256]{2,1,0:T(8,128)S(1)}, u32[]{:S(2)}, u32[]{:S(2)}) %collective-permute-start.5) | collective-permute-done | bytes 73760 | tf_op jit(solution)/shard_map/ppermute | solution.py:315
  34.4 0.0 copy-start.6
  34.4 0.0 collective-permute-done.4.refs_4_
  34.4 0.0 copy-start.1
  34.4 0.6 %copy-done.6 = f32[3,24,256]{2,1,0:T(8,128)} copy-done((f32[3,24,256]{2,1,0:T(8,128)}, f32[3,24,256]{2,1,0:T(8,128)S(1)}, u32[]{:S(2)}) %copy-start.6) | copy-done | bytes 73752
  35.0 0.1 copy-done.1
  35.1 4.1 %last_chain.1 = (f32[3,24,256]{2,1,0:T(8,128)}, f32[3,24,256]{2,1,0:T(8,128)}) custom-call(s32[1]{0:T(128)} %bitcast.refs_0_, f32[3,56,256]{2,1,0:T(8,128)} %get-tuple-element.7.refs_1_, f32[1,3,52,256]{3,2,1,0:T(8,128)} %bitcast.7, f32[3,24,256]{2,1,0:T(8,128)} %copy-done.6, f32[3,52,256]{2,1,0:T(8,128)} %copy-done.1, f32[4,24,256]{2,1,0:T(8,128)} %copy-done.5, ...), custom_call_target="tpu_custom_call" | custom-call | tf_op jit(solution)/shard_map/last_chain/pallas_call | solution.py:286
  (1 shorter events, 0.0 us)
Async XLA Ops:
  0.6 0.9 %copy-start.7 = (f32[24,256]{1,0:T(8,128)S(1)}, f32[24,256]{1,0:T(8,128)}, u32[]{:S(2)}) copy-start(f32[24,256]{1,0:T(8,128)} %param.5) | copy-start | bytes 73732
  1.6 13.1 %copy-start = (f32[4,24,256]{2,1,0:T(8,128)}, f32[4,24,256]{2,1,0:T(8,128)S(1)}, u32[]{:S(2)}) copy-start(f32[4,24,256]{2,1,0:T(8,128)S(1)} %pad_maximum_fusion.refs_3_.refs_7_) | copy-start | bytes 294916
  1.6 7.7 %collective-permute-start.3 = (f32[4,24,256]{2,1,0:T(8,128)S(1)}, f32[4,24,256]{2,1,0:T(8,128)S(1)}, u32[]{:S(2)}, u32[]{:S(2)}) collective-permute-start(f32[4,24,256]{2,1,0:T(8,128)S(1)} %pad_maximum_fusion.refs_3_.refs_7_), channel_id=1, source_target_pairs={{0,6},{1,7},{2,0},{3,1},{4,2},{5,3},{6,4},{7,5},{8,14},{9,15},{10,... | collective-permute-start | bytes 294920 | tf_op jit(solution)/shard_map/ppermute | solution.py:315
  6.7 4.7 %collective-permute-start.2 = (f32[4,24,256]{2,1,0:T(8,128)S(1)}, f32[4,24,256]{2,1,0:T(8,128)S(1)}, u32[]{:S(2)}, u32[]{:S(2)}) collective-permute-start(f32[4,24,256]{2,1,0:T(8,128)S(1)} %pad_maximum_fusion.refs_3_.refs_7_), channel_id=1, source_target_pairs={{0,7},{1,0},{2,1},{3,2},{4,3},{5,4},{6,5},{7,6},{8,15},{9,8},{10,9... | collective-permute-start | bytes 294920 | tf_op jit(solution)/shard_map/ppermute | solution.py:315
  6.7 5.8 %collective-permute-start.1 = (f32[4,24,256]{2,1,0:T(8,128)S(1)}, f32[4,24,256]{2,1,0:T(8,128)S(1)}, u32[]{:S(2)}, u32[]{:S(2)}) collective-permute-start(f32[4,24,256]{2,1,0:T(8,128)S(1)} %pad_maximum_fusion.refs_3_.refs_7_), channel_id=1, source_target_pairs={{0,1},{1,2},{2,3},{3,4},{4,5},{5,6},{6,7},{7,0},{8,9},{9,10},{10,1... | collective-permute-start | bytes 294920 | tf_op jit(solution)/shard_map/ppermute | solution.py:315
  7.2 7.4 %collective-permute-start = (f32[4,24,256]{2,1,0:T(8,128)S(1)}, f32[4,24,256]{2,1,0:T(8,128)S(1)}, u32[]{:S(2)}, u32[]{:S(2)}) collective-permute-start(f32[4,24,256]{2,1,0:T(8,128)S(1)} %pad_maximum_fusion.refs_3_.refs_7_), channel_id=1, source_target_pairs={{0,2},{1,3},{2,4},{3,5},{4,6},{5,7},{6,0},{7,1},{8,10},{9,11},{10,... | collective-permute-start | bytes 294920 | tf_op jit(solution)/shard_map/ppermute | solution.py:315
  9.3 5.4 %copy-start.2 = (f32[4,24,256]{2,1,0:T(8,128)}, f32[4,24,256]{2,1,0:T(8,128)S(1)}, u32[]{:S(2)}) copy-start(f32[4,24,256]{2,1,0:T(8,128)S(1)} %collective-permute-done.3.refs_5_.refs_9_) | copy-start | bytes 294916
  11.4 3.3 %copy-start.3 = (f32[4,24,256]{2,1,0:T(8,128)}, f32[4,24,256]{2,1,0:T(8,128)S(1)}, u32[]{:S(2)}) copy-start(f32[4,24,256]{2,1,0:T(8,128)S(1)} %collective-permute-done.2.refs_4_.refs_8_) | copy-start | bytes 294916
  12.6 2.1 %copy-start.4 = (f32[4,24,256]{2,1,0:T(8,128)}, f32[4,24,256]{2,1,0:T(8,128)S(1)}, u32[]{:S(2)}) copy-start(f32[4,24,256]{2,1,0:T(8,128)S(1)} %collective-permute-done.1.refs_2_.refs_6_) | copy-start | bytes 294916
  14.7 0.6 %copy-start.5 = (f32[4,24,256]{2,1,0:T(8,128)}, f32[4,24,256]{2,1,0:T(8,128)S(1)}, u32[]{:S(2)}) copy-start(f32[4,24,256]{2,1,0:T(8,128)S(1)} %collective-permute-done.refs_1_.refs_5_) | copy-start | bytes 294916
  24.3 10.0 %collective-permute-start.4 = (f32[3,52,256]{2,1,0:T(8,128)}, f32[3,52,256]{2,1,0:T(8,128)S(1)}, u32[]{:S(2)}, u32[]{:S(2)}) collective-permute-start(f32[3,52,256]{2,1,0:T(8,128)} %get-tuple-element.8), channel_id=1, source_target_pairs={{0,24},{1,25},{2,26},{3,27},{4,28},{5,29},{6,30},{7,31},{16,0},{17... | collective-permute-start | bytes 479240 | tf_op jit(solution)/shard_map/ppermute | solution.py:315
  28.7 5.7 %collective-permute-start.5 = (f32[3,24,256]{2,1,0:T(8,128)}, f32[3,24,256]{2,1,0:T(8,128)S(1)}, u32[]{:S(2)}, u32[]{:S(2)}) collective-permute-start(f32[3,24,256]{2,1,0:T(8,128)} %get-tuple-element.9), channel_id=1, source_target_pairs={{0,16},{1,17},{2,18},{3,19},{4,20},{5,21},{6,22},{7,23},{8,24},{9,... | collective-permute-start | bytes 221192 | tf_op jit(solution)/shard_map/ppermute | solution.py:315
  34.4 0.6 %copy-start.6 = (f32[3,24,256]{2,1,0:T(8,128)}, f32[3,24,256]{2,1,0:T(8,128)S(1)}, u32[]{:S(2)}) copy-start(f32[3,24,256]{2,1,0:T(8,128)S(1)} %collective-permute-done.5.refs_3_) | copy-start | bytes 221188
  34.4 0.7 %copy-start.1 = (f32[3,52,256]{2,1,0:T(8,128)}, f32[3,52,256]{2,1,0:T(8,128)S(1)}, u32[]{:S(2)}) copy-start(f32[3,52,256]{2,1,0:T(8,128)S(1)} %collective-permute-done.4.refs_4_) | copy-start | bytes 479236

commit v2 on v1

v2 whole, which is shorter than its diff:
```python
import jax
import jax.numpy as jnp
from jax import lax
from jax.experimental import pallas as pl
from jax.experimental.pallas import tpu as pltpu
from jax.sharding import PartitionSpec as P

STEPS = 8


gravity = 2.0
coriolis = 0.5
viscosity = 0.5
time_step = 0.04

LANES = 128
BLOCK = 8
VMEM = pl.BlockSpec(memory_space=pltpu.VMEM)
SMEM = pl.BlockSpec(memory_space=pltpu.SMEM)
VMEM_LIMIT = 8 * 2**20
FLOPS_PER_US = 500_000_000


def lanes():
    return lax.broadcasted_iota(jnp.int32, (BLOCK, LANES), 1)


def pick(tile, index):
    return jnp.take_along_axis(tile, index, axis=1, mode="promise_in_bounds")


def dealt(natural):
    tiles = len(natural)
    out = []
    for i in range(tiles):
        column = tiles * lanes() + i
        index = lax.rem(column, LANES)
        value = pick(natural[0], index)
        for p in range(1, tiles):
            value = jnp.where(column >= p * LANES, pick(natural[p], index), value)
        out.append(value)
    return out


def gathered(tiled):
    tiles = len(tiled)
    out = []
    for p in range(tiles):
        column = p * LANES + lanes()
        index = column // tiles
        which = lax.rem(column, tiles)
        value = pick(tiled[0], index)
        for i in range(1, tiles):
            value = jnp.where(which == i, pick(tiled[i], index), value)
        out.append(value)
    return out


def east(tiled):
    return tiled[1:] + [pltpu.roll(tiled[0], LANES - 1, 1)]


def west(tiled):
    return [pltpu.roll(tiled[-1], 1, 1)] + tiled[:-1]


def slopes(src, row, tiles):
    def rows(plane, by):
        return [src[plane, i, pl.ds(row + by, BLOCK), :] for i in range(tiles)]

    here = [rows(f, 0) for f in range(3)]
    north = [rows(f, 1) for f in range(4)]
    south = [rows(f, -1) for f in range(4)]
    flux = rows(4, 0)
    easts = [east(value) for value in here + [flux]]
    wests = [west(value) for value in here + [flux]]
    out = []
    for i in range(tiles):
        u, w = here[1][i], here[2][i]
        en, un, wn, fn = (north[f][i] for f in range(4))
        es, us, ws, fs = (south[f][i] for f in range(4))
        ee, ue, we, ge = (easts[f][i] for f in range(4))
        ew, uw, ww, gw = (wests[f][i] for f in range(4))
        rest_e = ((en + es) + (ee + ew)) - ((fn - fs) + (ge - gw))
        rest_u = ((un + us) - u * (un - us)) + ((ue + uw) - w * (ue - uw))
        rest_w = ((wn + ws) - u * (wn - ws)) + ((we + ww) - w * (we - ww))
        rest_u = rest_u + (w - (en - es))
        rest_w = rest_w - (u + (ee - ew))
        out.append((rest_e, rest_u, rest_w))
    return here, out


def own_factor(keep, i, row, size):
    kept = keep[i, pl.ds(row, BLOCK), :]
    ratio = size / time_step
    return kept if ratio == 1.0 else ratio * kept + (1.0 - ratio)


def store(ref, i, row, value):
    at = pl.ds(row, BLOCK)
    for f in range(3):
        ref[f, i, at, :] = value[f]
    height = 2.0 + value[0]
    ref[3, i, at, :] = height * value[1]
    ref[4, i, at, :] = height * value[2]


def first_stage(src, mid, keep, blocks, pad, size, tiles):
    for block in blocks:
        row = pad + BLOCK * block
        here, rest = slopes(src, row, tiles)
        for i in range(tiles):
            factor = own_factor(keep, i, row, size)
            value = []
            for f in range(3):
                own = (1.0 - 2.0 * size) if f == 0 else factor
                value.append(own * here[f][i] + (0.5 * size) * rest[i][f])
            store(mid, i, row, value)


def second_stage(src, mid, keep, blocks, pad, size, tiles, put):
    for block in blocks:
        row = pad + BLOCK * block
        here, rest = slopes(mid, row, tiles)
        for i in range(tiles):
            factor = own_factor(keep, i, row, size)
            olds, news = [], []
            for f in range(3):
                own = (1.0 - 2.0 * size) if f == 0 else factor
                old = src[f, i, pl.ds(row, BLOCK), :]
                olds.append(old)
                news.append(0.5 * ((old + own * here[f][i]) + (0.5 * size) * rest[i][f]))
            put(block, i, olds, news)


def clear(ref, planes, tiles, starts):
    for f in range(planes):
        for i in range(tiles):
            for row in starts:
                ref[f, i, pl.ds(row, BLOCK), :] = jnp.zeros((BLOCK, LANES), jnp.float32)


def copy_rows(target, source, tiles, row_count, to, start):
    for f in range(3):
        for i in range(tiles):
            for b in range(0, row_count, BLOCK):
                take = min(BLOCK, row_count - b)
                target[f, i, pl.ds(to + b, take), :] = source(f, i, start + b, take)


def copy_natural(target, source, tiles, row_count, start):
    for f in range(3):
        for b in range(0, row_count, BLOCK):
            tiled = [source(f, i, start + b, BLOCK) for i in range(tiles)]
            for p, value in enumerate(gathered(tiled)):
                target[f, pl.ds(b, BLOCK), pl.ds(p * LANES, LANES)] = 0.5 * value if f == 0 else value


def fine_kernel(layout, which_ref, *refs):
    count, strip, margin, tiles, slices, paired = layout
    parts = refs[: 2 * count + 1]
    narrow_ref, far_ref, wide_ref, factor_ref, state, mid, keep, before, coarse = refs[2 * count + 1 :]
    rows = (2 * count + 1) * strip
    pad = BLOCK
    centre = count * strip // BLOCK
    strip_blocks = range(centre, centre + strip // BLOCK)
    total = rows // BLOCK
    which = which_ref[0]

    for ref in (state, mid):
        clear(ref, 5, tiles, (0, pad + rows))

    def load(p, part):
        for b in range(0, strip, BLOCK):
            row = pad + p * strip + b
            if not isinstance(p, int):
                row = pl.multiple_of(row, BLOCK)
            if len(part.shape) == 4:
                planes = [[part[f, i, pl.ds(b, BLOCK), :] for i in range(tiles)] for f in range(4)]
            else:
                planes = dealt_block(part, b, tiles)
            for i in range(tiles):
                store(state, i, row, [planes[f][i] for f in range(3)])
                keep[i, pl.ds(row, BLOCK), :] = planes[3][i]

    for p, part in enumerate(parts):
        load(which_ref[1 + p] if paired and p != count else p, part)

    def put(block, i, olds, news):
        if block in strip_blocks:
            for f in range(3):
                before[f, i, pl.ds((block - centre) * BLOCK, BLOCK), :] = olds[f]
        store(state, i, pad + BLOCK * block, news)

    def steps(start, group):
        first, last = start // BLOCK, total - start // BLOCK

        def one(turn, carry):
            first_stage(state, mid, keep, range(first, last), pad, time_step, tiles)
            second_stage(state, mid, keep, range(first, last), pad, time_step, tiles, put)
            return carry

        lax.fori_loop(0, group, one, 0)

    def from_state(f, i, row, take):
        return state[f, i, pl.ds(pad + row, take), :]

    def from_before(f, i, row, take):
        return before[f, i, pl.ds(row, take), :]

    group = BLOCK // 2
    for start in range(0, STEPS, group):
        steps(2 * start, group)

    wide = strip + 2 * margin
    edge = count * strip - margin
    out_first, out_last = edge // BLOCK, (edge + wide) // BLOCK

    @pl.when(which == slices - 2)
    def _():
        copy_natural(narrow_ref, from_state, tiles, strip, count * strip)

    @pl.when(which == slices - 1)
    def _():
        copy_rows(far_ref, from_before, tiles, strip, 0, 0)

    def put_coarse(block, i, olds, news):
        for f in range(3):
            coarse[f, i, pl.ds((block - out_first) * BLOCK, BLOCK), :] = news[f]

    size = STEPS * time_step
    first_stage(state, mid, keep, range(out_first - 1, out_last + 1), pad, size, tiles)
    second_stage(state, mid, keep, range(out_first, out_last), pad, size, tiles, put_coarse)

    for start in range(STEPS, 2 * STEPS, group):
        steps(2 * start, group)

    def from_defect(f, i, row, take):
        return state[f, i, pl.ds(pad + row, take), :] - coarse[f, i, pl.ds(row - edge, take), :]

    for i in range(tiles):
        for b in range(0, wide + 2 * pad, BLOCK):
            factor_ref[i, pl.ds(b, BLOCK), :] = keep[i, pl.ds(edge + b, BLOCK), :]

    @pl.when(which < slices - 2)
    def _():
        copy_natural(narrow_ref, from_defect, tiles, strip, count * strip)
        copy_rows(far_ref, from_defect, tiles, wide - 4, 0, edge + 2)
        copy_rows(wide_ref, from_defect, tiles, wide, 0, edge)

    @pl.when(which >= slices - 2)
    def _():
        copy_rows(wide_ref, from_state, tiles, wide, 0, edge)

    @pl.when(which == slices - 2)
    def _():
        copy_rows(far_ref, from_before, tiles, strip, 0, 0)

    @pl.when(which == slices - 1)
    def _():
        copy_natural(narrow_ref, from_state, tiles, strip, count * strip)


def array(*shape):
    return jax.ShapeDtypeStruct(shape, jnp.float32)


def scratch(*shape):
    return pltpu.VMEM(shape, jnp.float32)


def call(kernel, name, micros, out_shape, args, scratches=()):
    return pl.pallas_call(
        kernel,
        name=name,
        out_shape=out_shape,
        in_specs=[SMEM] + [VMEM] * (len(args) - 1),
        out_specs=tuple(VMEM for _ in out_shape),
        scratch_shapes=list(scratches),
        compiler_params=pltpu.CompilerParams(vmem_limit_bytes=VMEM_LIMIT),
        cost_estimate=pl.CostEstimate(flops=int(micros * FLOPS_PER_US), bytes_accessed=0, transcendentals=0),
    )(*args)


def dealt_block(ref, b, tiles):
    out = []
    for f in range(4):
        tiled = dealt([ref[f, pl.ds(b, BLOCK), pl.ds(p * LANES, LANES)] for p in range(tiles)])
        if f == 0:
            tiled = [2.0 * value for value in tiled]
        if f == 3:
            tiled = [(1.0 - 2.0 * time_step) - time_step * value for value in tiled]
        out.append(tiled)
    return out


def deal_kernel(tiles, which_ref, *refs):
    half = len(refs) // 2
    for ref, out_ref in zip(refs[:half], refs[half:]):
        for b in range(0, ref.shape[1], BLOCK):
            for f, tiled in enumerate(dealt_block(ref, b, tiles)):
                for i, value in enumerate(tiled):
                    out_ref[f, i, pl.ds(b, BLOCK), :] = value


def deal(which, *parts):
    strip, columns = parts[0].shape[1:]
    tiles = columns // LANES
    out = tuple(array(4, tiles, strip, LANES) for _ in parts)
    return call(lambda *refs: deal_kernel(tiles, *refs), "deal", 0.5, out, [which, *parts])


def fine_chain(which, parts, margin, slices, paired):
    count = len(parts) // 2
    tiles, strip = parts[0].shape[1:3]
    wide = strip + 2 * margin
    rows = len(parts) * strip + 2 * BLOCK
    layout = (count, strip, margin, tiles, slices, paired)
    return call(
        lambda *refs: fine_kernel(layout, *refs),
        "fine_chain",
        8,
        (
            array(3, strip, tiles * LANES),
            array(3, tiles, wide - 4, LANES),
            array(3, tiles, wide, LANES),
            array(tiles, wide + 2 * BLOCK, LANES),
        ),
        [which, *parts],
        [
            scratch(5, tiles, rows, LANES),
            scratch(5, tiles, rows, LANES),
            scratch(tiles, rows, LANES),
            scratch(3, tiles, strip, LANES),
            scratch(3, tiles, wide, LANES),
        ],
    )


def widen(state, wide_ref, wide, tiles, pad):
    clear(state, 5, tiles, (0, pad + wide))
    for i in range(tiles):
        for b in range(0, wide, BLOCK):
            store(state, i, pad + b, [wide_ref[f, i, pl.ds(b, BLOCK), :] for f in range(3)])


def link_kernel(tiles, which_ref, wide_ref, keep, out_ref, state, mid):
    wide = wide_ref.shape[2]
    pad = BLOCK
    total = wide // BLOCK
    size = STEPS * time_step
    clear(mid, 5, tiles, (0, pad + wide))

    def put(block, i, olds, news):
        for f in range(3):
            out_ref[f, i, pl.ds(BLOCK * block, BLOCK), :] = news[f]

    linked = which_ref[0] > 2

    @pl.when(linked)
    def _():
        widen(state, wide_ref, wide, tiles, pad)
        first_stage(state, mid, keep, range(total), pad, size, tiles)
        second_stage(state, mid, keep, range(total), pad, size, tiles, put)

    @pl.when(jnp.logical_not(linked))
    def _():
        copy_rows(out_ref, lambda f, i, row, take: wide_ref[f, i, pl.ds(row, take), :], tiles, wide, 0, 0)


def first_link(which, wide, keep):
    tiles, rows = wide.shape[1:3]
    padded = (5, tiles, rows + 2 * BLOCK, LANES)
    return call(
        lambda *refs: link_kernel(tiles, *refs),
        "first_link",
        1,
        (array(*wide.shape),),
        [which, wide, keep],
        [scratch(*padded), scratch(*padded)],
    )[0]


def last_kernel(layout, which_ref, start_ref, keep, far_ref, *refs):
    strip, margin, tiles, chain = layout
    more_refs = refs[:-4]
    c_ref, f_ref, state, mid = refs[-4:]
    wide = strip + 2 * margin
    pad = BLOCK
    which = which_ref[0]
    total = wide // BLOCK
    coarse_size = STEPS * time_step

    clear(mid, 5, tiles, (0, pad + wide))

    def put(block, i, olds, news):
        store(state, i, pad + BLOCK * block, news)

    def add(defect, start_from):
        for f in range(3):
            for i in range(tiles):
                for b in range(0, wide - 4, BLOCK):
                    take = min(BLOCK, wide - 4 - b)
                    at = pl.ds(pad + 2 + b, take)
                    state[f, i, at, :] = start_from(f, i, 2 + b, take) + defect(f, i, b, take)
        for i in range(tiles):
            for b in range(0, wide, BLOCK):
                at = pl.ds(pad + b, BLOCK)
                height = 2.0 + state[0, i, at, :]
                state[3, i, at, :] = height * state[1, i, at, :]
                state[4, i, at, :] = height * state[2, i, at, :]

    def of_start(f, i, row, take):
        return start_ref[f, i, pl.ds(row, take), :]

    def of_state(f, i, row, take):
        return state[f, i, pl.ds(pad + row, take), :]

    def of_rows(ref):
        return lambda f, i, row, take: ref[f, i, pl.ds(row, take), :]

    def link(turn):
        if turn:
            first_stage(state, mid, keep, range(total), pad, coarse_size, tiles)
            second_stage(state, mid, keep, range(total), pad, coarse_size, tiles, put)
        defect = of_rows(more_refs[0].at[turn]) if more_refs else of_rows(far_ref)
        add(defect, of_state if turn else of_start)

    for turn in range(chain):
        pl.when(which > turn + 2)(lambda turn=turn: link(turn))
    pl.when(which <= 2)(lambda: widen(state, start_ref, wide, tiles, pad))

    first = margin // BLOCK
    strip_blocks = range(first, first + strip // BLOCK)

    early = which < 2

    def put_to(ref, value_of):
        def put_one(block, i, olds, news):
            at = pl.ds((block - first) * BLOCK, BLOCK)
            for f in range(3):
                value = value_of(f, i, at, news[f])
                ready[f].append(0.5 * value if f == 0 else value)
                if len(ready[f]) == tiles:
                    for p, natural in enumerate(gathered(ready[f])):
                        ref[f, at, pl.ds(p * LANES, LANES)] = natural
                    ready[f].clear()

        ready = [[], [], []]
        return put_one

    def c_value(f, i, at, new):
        return new

    def f_value(f, i, at, new):
        return jnp.where(early, far_ref[f, i, at, :], new)

    around = range(first - 1, first + strip // BLOCK + 1)
    first_stage(state, mid, keep, around, pad, coarse_size, tiles)
    second_stage(state, mid, keep, strip_blocks, pad, coarse_size, tiles, put_to(c_ref, c_value))

    def steps(blocks, group):
        def one(turn, carry):
            first_stage(state, mid, keep, blocks, pad, time_step, tiles)
            second_stage(state, mid, keep, blocks, pad, time_step, tiles, put)
            return carry

        if group > 0:
            lax.fori_loop(0, group, one, 0)

    near = min(BLOCK // 2 - 1, STEPS - 2)
    steps(range(total), STEPS - 2 - near)
    steps(around, near)
    first_stage(state, mid, keep, around, pad, time_step, tiles)
    second_stage(state, mid, keep, strip_blocks, pad, time_step, tiles, put_to(f_ref, f_value))


def last_chain(which, start, keep, far, more, strip, margin):
    tiles = start.shape[1]
    chain = more[0].shape[0] if more else 1
    layout = (strip, margin, tiles, chain)
    padded = (5, tiles, start.shape[2] + 2 * BLOCK, LANES)
    return call(
        lambda *refs: last_kernel(layout, *refs),
        "last_chain",
        3,
        (array(3, strip, tiles * LANES), array(3, strip, tiles * LANES)),
        [which, start, keep, far, *more],
        [scratch(*padded), scratch(*padded)],
    )


def body(initial_state, c_guess, friction):
    slices, strips = lax.axis_size("tm"), lax.axis_size("space")
    strip = initial_state.shape[1]
    which = lax.axis_index("tm")
    margin = 2 * (STEPS - 1) + 2 * (slices - 3)
    count = -(-(4 * STEPS + margin) // strip)
    both = ("tm", "space")

    def moved(value, target):
        pairs = []
        for t in range(slices):
            for s in range(strips):
                to = target(t, s)
                if to is not None:
                    pairs.append((t * strips + s, to[0] * strips + to[1] % strips))
        return lax.ppermute(value, both, pairs)

    place = lax.axis_index("space")
    paired = count == 2 and strips % 4 == 0
    side, turn = place % 2, place // 2 % 2
    spots = [4 - 4 * turn, 1 + 2 * side, jnp.full_like(side, 2), 3 - 2 * side, 4 * turn]
    index = jnp.stack([which, *spots]).astype(jnp.int32)
    start = jnp.where(which >= slices - 2, initial_state, c_guess[0])
    own = jnp.concatenate([start, friction[None]], axis=0)
    if paired:
        partner = moved(own, lambda t, s: (t, s ^ 1))
        one = moved(own, lambda t, s: (t, s ^ 2))
        other = moved(own, lambda t, s: (t, s - 2 if s // 2 % 2 == 0 else s + 2))
        relayed = moved(jnp.where(side == turn, one, other), lambda t, s: (t, s ^ 1))
        own, partner = deal(index, own, partner)
        one, other = deal(index, one, other)
        parts = [one, relayed, own, partner, other]
    else:
        parts = []
        for offset in range(-count, count + 1):
            parts.append(own if offset == 0 else moved(own, lambda t, s, o=offset: (t, s - o)))
        parts = list(deal(index, *parts))
    narrow, far, wide, keep = fine_chain(index, parts, margin, slices, paired)

    got_far = moved(far, lambda t, s: (slices - 1 - t, s))
    got = moved(narrow, lambda t, s: ((t + 2) % slices, s))
    more = []
    if slices != 4:
        everyone = lax.all_gather(wide, "tm", axis=0)
        more = [everyone[: slices - 3, :, :, 2:-2]]
        wide = everyone[slices - 1]
    first = first_link(index, wide, keep)
    coarse, f_points = last_chain(index, first, keep, got_far, more, strip, margin)
    c_points = jnp.where(which < 2, got, coarse + got)
    return (c_points[None], f_points[None])


def solution(mesh):
    placed = (P(None, "space", None), P("tm", None, "space", None), P("space", None))
    return jax.shard_map(
        body,
        mesh=mesh,
        in_specs=placed,
        out_specs=(P("tm", None, "space", None), P("tm", None, "space", None)),
        check_vma=False,
    )
```

time: 39.4 us -> 32.7 us (0.83)
  waiting for transfers between devices: 12.3 us -> 9.18 us
  starting transfers between devices: 10.7 us -> 8.33 us
  local copies, waits for them, and re-layouts: 1.32 us -> 0.09 us
  other arithmetic: 0.91 us -> 1.57 us
  Pallas kernels: 13.1 us -> 12.6 us
    ppermute x6, waiting for transfers between devices: 12.3 us -> 9.18 us  [moved(): return lax.ppermute(value, both, pairs)]
    ppermute x6, starting transfers between devices: 10.7 us -> 8.33 us  [moved(): return lax.ppermute(value, both, pairs)]
    unnamed x16 -> x2, local copies, waits for them, and re-layouts: 1.32 us -> 0.01 us
    broadcast_in_dim x0 -> x1, other arithmetic: none -> 0.64 us  [body(): return (c_points[None], f_points[None])]
    pallas_call x2 -> x5, Pallas kernels: 13.1 us -> 12.6 us  [call(): pl.pallas_call(kernel, name=name, out_shape=out_shape, in_specs=[SMEM] +...]
  transfers between devices with their start and end apart: 6 -> 6, of which waited for: 5 -> 3; matrix products, arithmetic and copies ran while one was open for 0% -> 0% of each run, Pallas kernels for 0% -> 17%
where the time goes in v2:
time: 32.7 us; the launch traced here: 32.5 us
  Pallas kernels  12.6 us (39%)
  waiting for transfers between devices  9.18 us (28%)
  starting transfers between devices  8.33 us (25%)
  other arithmetic  1.57 us (5%)
  between operations  0.73 us (2%)
    pallas_call x5, Pallas kernels, call(): pl.pallas_call(kernel, name=name, out_shape=out_shape, in_specs=[SMEM] +...  12.6 us
    ppermute x6, waiting for transfers between devices, moved(): return lax.ppermute(value, both, pairs)  9.18 us
    ppermute x6, starting transfers between devices, moved(): return lax.ppermute(value, both, pairs)  8.33 us
    select_n x1, other arithmetic, body(): start = jnp.where(which >= slices - 2, initial_state, c_guess[0])  0.9 us
  transfers between devices with their start and end apart: 6, of which 3 were waited for; matrix products, arithmetic and copies ran while one was open for 0% of the time, Pallas kernels for 17%

profile of v2, /device:TPU:0, one launch (start us, length us, event | category | flops | bytes accessed | tf_op | source)
XLA Modules:
  0.0 32.5 jit_solution(1383690528347955925)
XLA Ops:
  0.6 0.0 copy-start
  0.6 0.9 %bitcast_select_fusion = f32[3,24,256]{2,1,0:T(8,128)S(1)} fusion(f32[3,24,256]{2,1,0:T(8,128)} %param.3, f32[1,3,24,256]{3,2,1,0:T(8,128)} %param.4, pred[]{:T(512)S(6)} %ge.3), kind=kLoop, calls=%fused_computation.3 | loop fusion | flops 18432 | bytes 221185 | tf_op jit(solution)/shard_map/jit(_where)/select_n | solution.py:515
  1.6 0.0 copy-done
  1.6 5.1 %collective-permute-start.1 = (f32[4,24,256]{2,1,0:T(8,128)S(1)}, f32[4,24,256]{2,1,0:T(8,128)S(1)}, u32[]{:S(2)}, u32[]{:S(2)}) collective-permute-start(f32[4,24,256]{2,1,0:T(8,128)S(1)} %pad_maximum_fusion.refs_1_), channel_id=1, source_target_pairs={{0,6},{1,7},{2,4},{3,5},{4,2},{5,3},{6,0},{7,1},{8,14},{9,15},{10,... | collective-permute-start | bytes 294920 | tf_op jit(solution)/shard_map/ppermute | solution.py:508
  6.7 0.0 collective-permute-start
  6.7 0.0 collective-permute-start.3
  6.7 3.7 %collective-permute-done.1.refs_2_ = f32[4,24,256]{2,1,0:T(8,128)S(1)} collective-permute-done((f32[4,24,256]{2,1,0:T(8,128)S(1)}, f32[4,24,256]{2,1,0:T(8,128)S(1)}, u32[]{:S(2)}, u32[]{:S(2)}) %collective-permute-start.1) | collective-permute-done | bytes 98336 | tf_op jit(solution)/shard_map/ppermute | solution.py:508
  10.4 1.3 %collective-permute-done.refs_1_ = f32[4,24,256]{2,1,0:T(8,128)S(1)} collective-permute-done((f32[4,24,256]{2,1,0:T(8,128)S(1)}, f32[4,24,256]{2,1,0:T(8,128)S(1)}, u32[]{:S(2)}, u32[]{:S(2)}) %collective-permute-start) | collective-permute-done | bytes 98336 | tf_op jit(solution)/shard_map/ppermute | solution.py:508
  11.8 0.1 collective-permute-start.2
  11.9 0.1 stack.23.refs_0_
  11.9 0.8 %deal.2 = (f32[4,2,24,128]{3,2,1,0:T(8,128)S(1)}, f32[4,2,24,128]{3,2,1,0:T(8,128)S(1)}) custom-call(s32[6]{0:T(128)S(1)} %stack.23.refs_0_, f32[4,24,256]{2,1,0:T(8,128)S(1)} %collective-permute-done.refs_1_, f32[4,24,256]{2,1,0:T(8,128)S(1)} %collective-permute-done.1.refs_2_), custom_call_target="tpu_custom_call" | custom-call | flops 250000000 | tf_op jit(solution)/shard_map/deal/pallas_call | solution.py:273
  12.8 0.0 collective-permute-done.3.refs_2_
  12.8 0.8 %deal.3 = (f32[4,2,24,128]{3,2,1,0:T(8,128)S(1)}, f32[4,2,24,128]{3,2,1,0:T(8,128)S(1)}) custom-call(s32[6]{0:T(128)S(1)} %stack.23.refs_0_, f32[4,24,256]{2,1,0:T(8,128)S(1)} %pad_maximum_fusion.refs_1_, f32[4,24,256]{2,1,0:T(8,128)S(1)} %collective-permute-done.3.refs_2_), custom_call_target="tpu_custom_call" | custom-call | flops 250000000 | tf_op jit(solution)/shard_map/deal/pallas_call | solution.py:273
  13.6 0.0 collective-permute-done.2.refs_2_
  13.6 7.0 %fine_chain.1 = (f32[3,24,256]{2,1,0:T(8,128)S(1)}, f32[3,2,52,128]{3,2,1,0:T(8,128)S(1)}, f32[3,2,56,128]{3,2,1,0:T(8,128)S(1)}, f32[2,72,128]{2,1,0:T(8,128)S(1)}) custom-call(s32[6]{0:T(128)S(1)} %stack.23.refs_0_, f32[4,2,24,128]{3,2,1,0:T(8,128)S(1)} %get-tuple-element.12.refs_1_, f32[4,24,256]{2,1,0:T(8,128)S(1)} %collective-permute-done.2.refs_2_, ...), custom_call_target="tpu_custom_call" | custom-call | flops 4000000000 | tf_op jit(solution)/shard_map/fine_chain/pallas_call | solution.py:273
  20.7 2.6 %collective-permute-start.5 = (f32[3,2,52,128]{3,2,1,0:T(8,128)S(1)}, f32[3,2,52,128]{3,2,1,0:T(8,128)S(1)}, u32[]{:S(2)}, u32[]{:S(2)}) collective-permute-start(f32[3,2,52,128]{3,2,1,0:T(8,128)S(1)} %get-tuple-element.19), channel_id=1, source_target_pairs={{0,24},{1,25},{2,26},{3,27},{4,28},{5,29},{6,30},{7,31},{8,16},{9,... | collective-permute-start | bytes 479240 | tf_op jit(solution)/shard_map/ppermute | solution.py:508
  23.3 0.5 %collective-permute-start.4 = (f32[3,24,256]{2,1,0:T(8,128)S(1)}, f32[3,24,256]{2,1,0:T(8,128)S(1)}, u32[]{:S(2)}, u32[]{:S(2)}) collective-permute-start(f32[3,24,256]{2,1,0:T(8,128)S(1)} %get-tuple-element.16), channel_id=1, source_target_pairs={{0,16},{1,17},{2,18},{3,19},{4,20},{5,21},{6,22},{7,23},{8,24},{9,... | collective-permute-start | bytes 221192 | tf_op jit(solution)/shard_map/ppermute | solution.py:508
  23.8 0.6 %first_link.1.refs_1_ = f32[3,2,56,128]{3,2,1,0:T(8,128)S(1)} custom-call(s32[6]{0:T(128)S(1)} %stack.23.refs_0_, f32[3,2,56,128]{3,2,1,0:T(8,128)S(1)} %get-tuple-element.17.refs_1_, f32[2,72,128]{2,1,0:T(8,128)S(1)} %get-tuple-element.18.refs_2_), custom_call_target="tpu_custom_call" | custom-call | flops 500000000 | tf_op jit(solution)/shard_map/first_link/pallas_call | solution.py:273
  24.3 4.2 %collective-permute-done.5.refs_3_ = f32[3,2,52,128]{3,2,1,0:T(8,128)S(1)} collective-permute-done((f32[3,2,52,128]{3,2,1,0:T(8,128)S(1)}, f32[3,2,52,128]{3,2,1,0:T(8,128)S(1)}, u32[]{:S(2)}, u32[]{:S(2)}) %collective-permute-start.5) | collective-permute-done | bytes 159776 | tf_op jit(solution)/shard_map/ppermute | solution.py:508
  28.5 3.4 %last_chain.1 = (f32[3,24,256]{2,1,0:T(8,128)S(1)}, f32[3,24,256]{2,1,0:T(8,128)}) custom-call(s32[6]{0:T(128)S(1)} %stack.23.refs_0_, f32[3,2,56,128]{3,2,1,0:T(8,128)S(1)} %first_link.1.refs_1_, f32[2,72,128]{2,1,0:T(8,128)S(1)} %get-tuple-element.18.refs_2_, f32[3,2,52,128]{3,2,1,0:T(8,128)S(1)} %collective-permute-done.5.refs_3_), custom_call_target="tpu_custom_call" | custom-call | flops 1500000000 | tf_op jit(solution)/shard_map/last_chain/pallas_call | solution.py:273
  31.9 0.0 collective-permute-done.4
  31.9 0.6 %fusion = f32[1,3,24,256]{3,2,1,0:T(8,128)} fusion(f32[3,24,256]{2,1,0:T(8,128)S(1)} %collective-permute-done.4, f32[3,24,256]{2,1,0:T(8,128)S(1)} %get-tuple-element.20, pred[]{:T(512)S(6)} %lt.13), kind=kLoop, calls=%fused_computation.2 | loop fusion | flops 36864 | bytes 221185 | tf_op jit(solution)/shard_map/broadcast_in_dim | solution.py:542
  (2 shorter events, 0.0 us)
Async XLA Ops:
  0.6 0.9 %copy-start = (f32[24,256]{1,0:T(8,128)S(1)}, f32[24,256]{1,0:T(8,128)}, u32[]{:S(2)}) copy-start(f32[24,256]{1,0:T(8,128)} %param.5) | copy-start | bytes 73732
  1.6 8.8 %collective-permute-start.1 = (f32[4,24,256]{2,1,0:T(8,128)S(1)}, f32[4,24,256]{2,1,0:T(8,128)S(1)}, u32[]{:S(2)}, u32[]{:S(2)}) collective-permute-start(f32[4,24,256]{2,1,0:T(8,128)S(1)} %pad_maximum_fusion.refs_1_), channel_id=1, source_target_pairs={{0,6},{1,7},{2,4},{3,5},{4,2},{5,3},{6,0},{7,1},{8,14},{9,15},{10,... | collective-permute-start | bytes 294920 | tf_op jit(solution)/shard_map/ppermute | solution.py:508
  6.7 5.0 %collective-permute-start = (f32[4,24,256]{2,1,0:T(8,128)S(1)}, f32[4,24,256]{2,1,0:T(8,128)S(1)}, u32[]{:S(2)}, u32[]{:S(2)}) collective-permute-start(f32[4,24,256]{2,1,0:T(8,128)S(1)} %pad_maximum_fusion.refs_1_), channel_id=1, source_target_pairs={{0,2},{1,3},{2,0},{3,1},{4,6},{5,7},{6,4},{7,5},{8,10},{9,11},{10,... | collective-permute-start | bytes 294920 | tf_op jit(solution)/shard_map/ppermute | solution.py:508
  6.7 6.0 %collective-permute-start.3 = (f32[4,24,256]{2,1,0:T(8,128)S(1)}, f32[4,24,256]{2,1,0:T(8,128)S(1)}, u32[]{:S(2)}, u32[]{:S(2)}) collective-permute-start(f32[4,24,256]{2,1,0:T(8,128)S(1)} %pad_maximum_fusion.refs_1_), channel_id=1, source_target_pairs={{0,1},{1,0},{2,3},{3,2},{4,5},{5,4},{6,7},{7,6},{8,9},{9,8},{10,11... | collective-permute-start | bytes 294920 | tf_op jit(solution)/shard_map/ppermute | solution.py:508
  11.8 1.8 %collective-permute-start.2 = (f32[4,24,256]{2,1,0:T(8,128)S(1)}, f32[4,24,256]{2,1,0:T(8,128)S(1)}, u32[]{:S(2)}, u32[]{:S(2)}) collective-permute-start(f32[4,24,256]{2,1,0:T(8,128)S(1)} %broadcast_select_fusion), channel_id=1, source_target_pairs={{0,1},{1,0},{2,3},{3,2},{4,5},{5,4},{6,7},{7,6},{8,9},{9,8},{10,11... | collective-permute-start | bytes 294920 | tf_op jit(solution)/shard_map/ppermute | solution.py:508
  20.7 7.8 %collective-permute-start.5 = (f32[3,2,52,128]{3,2,1,0:T(8,128)S(1)}, f32[3,2,52,128]{3,2,1,0:T(8,128)S(1)}, u32[]{:S(2)}, u32[]{:S(2)}) collective-permute-start(f32[3,2,52,128]{3,2,1,0:T(8,128)S(1)} %get-tuple-element.19), channel_id=1, source_target_pairs={{0,24},{1,25},{2,26},{3,27},{4,28},{5,29},{6,30},{7,31},{8,16},{9,... | collective-permute-start | bytes 479240 | tf_op jit(solution)/shard_map/ppermute | solution.py:508
  23.3 8.6 %collective-permute-start.4 = (f32[3,24,256]{2,1,0:T(8,128)S(1)}, f32[3,24,256]{2,1,0:T(8,128)S(1)}, u32[]{:S(2)}, u32[]{:S(2)}) collective-permute-start(f32[3,24,256]{2,1,0:T(8,128)S(1)} %get-tuple-element.16), channel_id=1, source_target_pairs={{0,16},{1,17},{2,18},{3,19},{4,20},{5,21},{6,22},{7,23},{8,24},{9,... | collective-permute-start | bytes 221192 | tf_op jit(solution)/shard_map/ppermute | solution.py:508

commit v3 on v2

--- a/solution.py
+++ b/solution.py
@@ -16,7 +16,6 @@
 LANES = 128
 BLOCK = 8
 VMEM = pl.BlockSpec(memory_space=pltpu.VMEM)
-SMEM = pl.BlockSpec(memory_space=pltpu.SMEM)
 VMEM_LIMIT = 8 * 2**20
 FLOPS_PER_US = 500_000_000
 
@@ -156,16 +155,16 @@
                 target[f, pl.ds(b, BLOCK), pl.ds(p * LANES, LANES)] = 0.5 * value if f == 0 else value
 
 
-def fine_kernel(layout, which_ref, *refs):
+def fine_kernel(layout, standing_at, *refs):
     count, strip, margin, tiles, slices, paired = layout
     parts = refs[: 2 * count + 1]
-    narrow_ref, far_ref, wide_ref, factor_ref, state, mid, keep, before, coarse = refs[2 * count + 1 :]
+    far_ref, raw_ref, start_ref, relaxed_ref, coarse, factor_ref, state, mid, keep, before = refs[2 * count + 1 :]
     rows = (2 * count + 1) * strip
     pad = BLOCK
     centre = count * strip // BLOCK
     strip_blocks = range(centre, centre + strip // BLOCK)
     total = rows // BLOCK
-    which = which_ref[0]
+    which = standing_at[0]
 
     for ref in (state, mid):
         clear(ref, 5, tiles, (0, pad + rows))
@@ -184,7 +183,7 @@
                 keep[i, pl.ds(row, BLOCK), :] = planes[3][i]
 
     for p, part in enumerate(parts):
-        load(which_ref[1 + p] if paired and p != count else p, part)
+        load(standing_at[1 + p] if paired and p != count else p, part)
 
     def put(block, i, olds, news):
         if block in strip_blocks:
@@ -208,17 +207,19 @@
     def from_before(f, i, row, take):
         return before[f, i, pl.ds(row, take), :]
 
+    wide = strip + 2 * margin
+    edge = count * strip - margin
+    out_first, out_last = edge // BLOCK, (edge + wide) // BLOCK
+    window = wide + 2 * BLOCK
+    for i in range(tiles):
+        for b in range(0, window + 2 * pad, BLOCK):
+            factor_ref[i, pl.ds(b, BLOCK), :] = keep[i, pl.ds(edge - BLOCK + b, BLOCK), :]
+    copy_rows(start_ref, from_state, tiles, window, 0, edge - BLOCK)
+
     group = BLOCK // 2
     for start in range(0, STEPS, group):
         steps(2 * start, group)
-
-    wide = strip + 2 * margin
-    edge = count * strip - margin
-    out_first, out_last = edge // BLOCK, (edge + wide) // BLOCK
-
-    @pl.when(which == slices - 2)
-    def _():
-        copy_natural(narrow_ref, from_state, tiles, strip, count * strip)
+    copy_rows(relaxed_ref, from_state, tiles, window, 0, edge - BLOCK)
 
     @pl.when(which == slices - 1)
     def _():
@@ -238,27 +239,18 @@
     def from_defect(f, i, row, take):
         return state[f, i, pl.ds(pad + row, take), :] - coarse[f, i, pl.ds(row - edge, take), :]
 
-    for i in range(tiles):
-        for b in range(0, wide + 2 * pad, BLOCK):
-            factor_ref[i, pl.ds(b, BLOCK), :] = keep[i, pl.ds(edge + b, BLOCK), :]
-
     @pl.when(which < slices - 2)
     def _():
-        copy_natural(narrow_ref, from_defect, tiles, strip, count * strip)
         copy_rows(far_ref, from_defect, tiles, wide - 4, 0, edge + 2)
-        copy_rows(wide_ref, from_defect, tiles, wide, 0, edge)
+        copy_rows(raw_ref, from_defect, tiles, wide, 0, edge)
 
     @pl.when(which >= slices - 2)
     def _():
-        copy_rows(wide_ref, from_state, tiles, wide, 0, edge)
+        copy_rows(raw_ref, from_state, tiles, wide, 0, edge)
 
     @pl.when(which == slices - 2)
     def _():
         copy_rows(far_ref, from_before, tiles, strip, 0, 0)
-
-    @pl.when(which == slices - 1)
-    def _():
-        copy_natural(narrow_ref, from_state, tiles, strip, count * strip)
 
 
 def array(*shape):
@@ -269,12 +261,18 @@
     return pltpu.VMEM(shape, jnp.float32)
 
 
+def standing():
+    place = lax.axis_index("space")
+    side, turn = lax.rem(place, 2), lax.rem(lax.div(place, 2), 2)
+    return [lax.axis_index("tm"), 4 - 4 * turn, 1 + 2 * side, 2, 3 - 2 * side, 4 * turn]
+
+
 def call(kernel, name, micros, out_shape, args, scratches=()):
     return pl.pallas_call(
-        kernel,
+        lambda *refs: kernel(standing(), *refs),
         name=name,
         out_shape=out_shape,
-        in_specs=[SMEM] + [VMEM] * (len(args) - 1),
+        in_specs=[VMEM] * len(args),
         out_specs=tuple(VMEM for _ in out_shape),
         scratch_shapes=list(scratches),
         compiler_params=pltpu.CompilerParams(vmem_limit_bytes=VMEM_LIMIT),
@@ -294,7 +292,7 @@
     return out
 
 
-def deal_kernel(tiles, which_ref, *refs):
+def deal_kernel(tiles, standing_at, *refs):
     half = len(refs) // 2
     for ref, out_ref in zip(refs[:half], refs[half:]):
         for b in range(0, ref.shape[1], BLOCK):
@@ -303,14 +301,14 @@
                     out_ref[f, i, pl.ds(b, BLOCK), :] = value
 
 
-def deal(which, *parts):
+def deal(*parts):
     strip, columns = parts[0].shape[1:]
     tiles = columns // LANES
     out = tuple(array(4, tiles, strip, LANES) for _ in parts)
-    return call(lambda *refs: deal_kernel(tiles, *refs), "deal", 0.5, out, [which, *parts])
-
-
-def fine_chain(which, parts, margin, slices, paired):
+    return call(lambda *refs: deal_kernel(tiles, *refs), "deal", 0.5, out, list(parts))
+
+
+def fine_chain(parts, margin, slices, paired):
     count = len(parts) // 2
     tiles, strip = parts[0].shape[1:3]
     wide = strip + 2 * margin
@@ -321,18 +319,19 @@
         "fine_chain",
         8,
         (
-            array(3, strip, tiles * LANES),
             array(3, tiles, wide - 4, LANES),
             array(3, tiles, wide, LANES),
-            array(tiles, wide + 2 * BLOCK, LANES),
+            array(3, tiles, wide + 2 * BLOCK, LANES),
+            array(3, tiles, wide + 2 * BLOCK, LANES),
+            array(3, tiles, wide, LANES),
+            array(tiles, wide + 4 * BLOCK, LANES),
         ),
-        [which, *parts],
+        list(parts),
         [
             scratch(5, tiles, rows, LANES),
             scratch(5, tiles, rows, LANES),
             scratch(tiles, rows, LANES),
             scratch(3, tiles, strip, LANES),
-            scratch(3, tiles, wide, LANES),
         ],
     )
 
@@ -344,18 +343,84 @@
             store(state, i, pad + b, [wide_ref[f, i, pl.ds(b, BLOCK), :] for f in range(3)])
 
 
-def link_kernel(tiles, which_ref, wide_ref, keep, out_ref, state, mid):
+def settle_kernel(layout, standing_at, raw_ref, start_ref, relaxed_ref, coarse_ref, keep, *refs):
+    narrow_ref, wide_ref, state, mid = refs
+    strip, margin, tiles, slices = layout
+    wide = strip + 2 * margin
+    window = wide + 2 * BLOCK
+    pad = BLOCK
+    total = window // BLOCK
+    which = standing_at[0]
+    size = STEPS * time_step
+
+    def rows_of(ref, lift=0):
+        return lambda f, i, row, take: ref[f, i, pl.ds(lift + row, take), :]
+
+    def put_first(block, i, olds, news):
+        at = pl.ds(BLOCK * block, BLOCK)
+        first = [news[f] + (relaxed_ref[f, i, at, :] - news[f]) for f in range(3)]
+        store(state, i, pad + BLOCK * block, first)
+
+    def put_second(block, i, olds, news):
+        at = pl.ds(BLOCK * (block - 1), BLOCK)
+        for f in range(3):
+            wide_ref[f, i, at, :] = news[f] + (raw_ref[f, i, at, :] - coarse_ref[f, i, at, :])
+
+    @pl.when(which < slices - 2)
+    def _():
+        copy_rows(wide_ref, rows_of(raw_ref), tiles, wide, 0, 0)
+        copy_natural(narrow_ref, rows_of(raw_ref), tiles, strip, margin)
+
+    @pl.when(which >= slices - 2)
+    def _():
+        clear(mid, 5, tiles, (0, pad + window))
+        widen(state, start_ref, window, tiles, pad)
+        first_stage(state, mid, keep, range(total), pad, size, tiles)
+        second_stage(state, mid, keep, range(total), pad, size, tiles, put_first)
+
+        @pl.when(which == slices - 2)
+        def _():
+            copy_natural(narrow_ref, rows_of(state, pad), tiles, strip, BLOCK + margin)
+
+        first_stage(state, mid, keep, range(total), pad, size, tiles)
+        second_stage(state, mid, keep, range(1, total - 1), pad, size, tiles, put_second)
+
+        @pl.when(which == slices - 1)
+        def _():
+            copy_natural(narrow_ref, rows_of(wide_ref), tiles, strip, margin)
+
+
+def settle(raw, start, relaxed, coarse, keep, strip, margin, slices):
+    tiles, wide = raw.shape[1:3]
+    layout = (strip, margin, tiles, slices)
+    padded = (5, tiles, wide + 4 * BLOCK, LANES)
+    return call(
+        lambda *refs: settle_kernel(layout, *refs),
+        "settle",
+        1,
+        (array(3, strip, tiles * LANES), array(3, tiles, wide, LANES)),
+        [raw, start, relaxed, coarse, keep],
+        [scratch(*padded), scratch(*padded)],
+    )
+
+
+def inner(keep):
+    return keep.at[:, pl.ds(BLOCK, keep.shape[1] - 2 * BLOCK), :]
+
+
+def link_kernel(tiles, standing_at, wide_ref, keep, out_ref, state, mid):
     wide = wide_ref.shape[2]
     pad = BLOCK
     total = wide // BLOCK
     size = STEPS * time_step
+    keep = inner(keep)
     clear(mid, 5, tiles, (0, pad + wide))
 
     def put(block, i, olds, news):
         for f in range(3):
             out_ref[f, i, pl.ds(BLOCK * block, BLOCK), :] = news[f]
 
-    linked = which_ref[0] > 2
+    linked = standing_at[0] > 2
 
     @pl.when(linked)
     def _():
@@ -368,7 +433,7 @@
         copy_rows(out_ref, lambda f, i, row, take: wide_ref[f, i, pl.ds(row, take), :], tiles, wide, 0, 0)
 
 
-def first_link(which, wide, keep):
+def first_link(wide, keep):
     tiles, rows = wide.shape[1:3]
     padded = (5, tiles, rows + 2 * BLOCK, LANES)
     return call(
@@ -376,20 +441,21 @@
         "first_link",
         1,
         (array(*wide.shape),),
-        [which, wide, keep],
+        [wide, keep],
         [scratch(*padded), scratch(*padded)],
     )[0]
 
 
-def last_kernel(layout, which_ref, start_ref, keep, far_ref, *refs):
+def last_kernel(layout, standing_at, start_ref, keep, far_ref, *refs):
     strip, margin, tiles, chain = layout
     more_refs = refs[:-4]
     c_ref, f_ref, state, mid = refs[-4:]
     wide = strip + 2 * margin
     pad = BLOCK
-    which = which_ref[0]
+    which = standing_at[0]
     total = wide // BLOCK
     coarse_size = STEPS * time_step
+    keep = inner(keep)
 
     clear(mid, 5, tiles, (0, pad + wide))
 
@@ -475,7 +541,7 @@
     second_stage(state, mid, keep, strip_blocks, pad, time_step, tiles, put_to(f_ref, f_value))
 
 
-def last_chain(which, start, keep, far, more, strip, margin):
+def last_chain(start, keep, far, more, strip, margin):
     tiles = start.shape[1]
     chain = more[0].shape[0] if more else 1
     layout = (strip, margin, tiles, chain)
@@ -485,7 +551,7 @@
         "last_chain",
         3,
         (array(3, strip, tiles * LANES), array(3, strip, tiles * LANES)),
-        [which, start, keep, far, *more],
+        [start, keep, far, *more],
         [scratch(*padded), scratch(*padded)],
     )
 
@@ -510,8 +576,6 @@
     place = lax.axis_index("space")
     paired = count == 2 and strips % 4 == 0
     side, turn = place % 2, place // 2 % 2
-    spots = [4 - 4 * turn, 1 + 2 * side, jnp.full_like(side, 2), 3 - 2 * side, 4 * turn]
-    index = jnp.stack([which, *spots]).astype(jnp.int32)
     start = jnp.where(which >= slices - 2, initial_state, c_guess[0])
     own = jnp.concatenate([start, friction[None]], axis=0)
     if paired:
@@ -519,25 +583,25 @@
         one = moved(own, lambda t, s: (t, s ^ 2))
         other = moved(own, lambda t, s: (t, s - 2 if s // 2 % 2 == 0 else s + 2))
         relayed = moved(jnp.where(side == turn, one, other), lambda t, s: (t, s ^ 1))
-        own, partner = deal(index, own, partner)
-        one, other = deal(index, one, other)
+        own, partner, one, other = deal(own, partner, one, other)
         parts = [one, relayed, own, partner, other]
     else:
         parts = []
         for offset in range(-count, count + 1):
             parts.append(own if offset == 0 else moved(own, lambda t, s, o=offset: (t, s - o)))
-        parts = list(deal(index, *parts))
-    narrow, far, wide, keep = fine_chain(index, parts, margin, slices, paired)
+        parts = list(deal(*parts))
+    far, raw, begin, relaxed, stepped, keep = fine_chain(parts, margin, slices, paired)
 
     got_far = moved(far, lambda t, s: (slices - 1 - t, s))
+    narrow, wide = settle(raw, begin, relaxed, stepped, keep, strip, margin, slices)
     got = moved(narrow, lambda t, s: ((t + 2) % slices, s))
     more = []
     if slices != 4:
         everyone = lax.all_gather(wide, "tm", axis=0)
         more = [everyone[: slices - 3, :, :, 2:-2]]
         wide = everyone[slices - 1]
-    first = first_link(index, wide, keep)
-    coarse, f_points = last_chain(index, first, keep, got_far, more, strip, margin)
+    first = first_link(wide, keep)
+    coarse, f_points = last_chain(first, keep, got_far, more, strip, margin)
     c_points = jnp.where(which < 2, got, coarse + got)
     return (c_points[None], f_points[None])
 

time: 32.7 us -> 30.6 us (0.936)
  Pallas kernels: 12.6 us -> 9.86 us
  starting transfers between devices: 8.33 us -> 9.02 us
    pallas_call x5, Pallas kernels: 12.6 us -> 9.86 us  [call(): pl.pallas_call(lambda *refs: kernel(standing(), *refs), name=name, out_sh...]
    ppermute x6, starting transfers between devices: 8.33 us -> 9.02 us  [moved(): return lax.ppermute(value, both, pairs)]
  transfers between devices with their start and end apart: 6 -> 6, of which waited for: 3 -> 4; matrix products, arithmetic and copies ran while one was open for 0% -> 0% of each run, Pallas kernels for 17% -> 11%
where the time goes in v3:
time: 30.6 us; the launch traced here: 30.5 us
  Pallas kernels  9.86 us (32%)
  waiting for transfers between devices  9.33 us (30%)
  starting transfers between devices  9.02 us (29%)
  other arithmetic  1.57 us (5%)
  between operations  0.71 us (2%)
    pallas_call x5, Pallas kernels, call(): pl.pallas_call(lambda *refs: kernel(standing(), *refs), name=name, out_sh...  9.86 us
    ppermute x6, waiting for transfers between devices, moved(): return lax.ppermute(value, both, pairs)  9.33 us
    ppermute x6, starting transfers between devices, moved(): return lax.ppermute(value, both, pairs)  9.02 us
    select_n x1, other arithmetic, body(): start = jnp.where(which >= slices - 2, initial_state, c_guess[0])  0.9 us
    broadcast_in_dim x1, other arithmetic, body(): return (c_points[None], f_points[None])  0.65 us
  transfers between devices with their start and end apart: 6, of which 4 were waited for; matrix products, arithmetic and copies ran while one was open for 0% of the time, Pallas kernels for 11%

profile of v3, /device:TPU:0, one launch (start us, length us, event | category | flops | bytes accessed | tf_op | source)
XLA Modules:
  0.0 30.5 jit_solution(4781945216060313807)
XLA Ops:
  0.6 0.0 copy-start
  0.6 0.9 %bitcast_select_fusion = f32[3,24,256]{2,1,0:T(8,128)S(1)} fusion(f32[3,24,256]{2,1,0:T(8,128)} %param.3, f32[1,3,24,256]{3,2,1,0:T(8,128)} %param.4, pred[]{:T(512)S(6)} %ge.3), kind=kLoop, calls=%fused_computation.3 | loop fusion | flops 18432 | bytes 221185 | tf_op jit(solution)/shard_map/jit(_where)/select_n | solution.py:579
  1.6 0.0 copy-done
  1.6 5.1 %collective-permute-start.2 = (f32[4,24,256]{2,1,0:T(8,128)S(1)}, f32[4,24,256]{2,1,0:T(8,128)S(1)}, u32[]{:S(2)}, u32[]{:S(2)}) collective-permute-start(f32[4,24,256]{2,1,0:T(8,128)S(1)} %pad_maximum_fusion.refs_0_), channel_id=1, source_target_pairs={{0,6},{1,7},{2,4},{3,5},{4,2},{5,3},{6,0},{7,1},{8,14},{9,15},{10,... | collective-permute-start | bytes 294920 | tf_op jit(solution)/shard_map/ppermute | solution.py:574
  6.7 0.0 collective-permute-start.1
  6.7 0.0 collective-permute-start
  6.7 3.7 %collective-permute-done.2.refs_3_ = f32[4,24,256]{2,1,0:T(8,128)S(1)} collective-permute-done((f32[4,24,256]{2,1,0:T(8,128)S(1)}, f32[4,24,256]{2,1,0:T(8,128)S(1)}, u32[]{:S(2)}, u32[]{:S(2)}) %collective-permute-start.2) | collective-permute-done | bytes 98336 | tf_op jit(solution)/shard_map/ppermute | solution.py:574
  10.4 1.3 %collective-permute-done.1.refs_2_ = f32[4,24,256]{2,1,0:T(8,128)S(1)} collective-permute-done((f32[4,24,256]{2,1,0:T(8,128)S(1)}, f32[4,24,256]{2,1,0:T(8,128)S(1)}, u32[]{:S(2)}, u32[]{:S(2)}) %collective-permute-start.1) | collective-permute-done | bytes 98336 | tf_op jit(solution)/shard_map/ppermute | solution.py:574
  11.8 0.1 collective-permute-start.3
  11.8 0.0 collective-permute-done.refs_1_
  11.9 0.5 %deal.1 = (f32[4,2,24,128]{3,2,1,0:T(8,128)S(1)}, f32[4,2,24,128]{3,2,1,0:T(8,128)S(1)}, f32[4,2,24,128]{3,2,1,0:T(8,128)S(1)}, f32[4,2,24,128]{3,2,1,0:T(8,128)S(1)}) custom-call(f32[4,24,256]{2,1,0:T(8,128)S(1)} %pad_maximum_fusion.refs_0_, f32[4,24,256]{2,1,0:T(8,128)S(1)} %collective-permute-done.refs_1_, ...), custom_call_target="tpu_custom_call" | custom-call | flops 250000000 | tf_op jit(solution)/shard_map/deal/pallas_call | solution.py:271
  12.4 0.8 %collective-permute-done.3.refs_1_ = f32[4,24,256]{2,1,0:T(8,128)S(1)} collective-permute-done((f32[4,24,256]{2,1,0:T(8,128)S(1)}, f32[4,24,256]{2,1,0:T(8,128)S(1)}, u32[]{:S(2)}, u32[]{:S(2)}) %collective-permute-start.3) | collective-permute-done | bytes 98336 | tf_op jit(solution)/shard_map/ppermute | solution.py:574
  13.1 6.4 %fine_chain.1 = (f32[3,2,52,128]{3,2,1,0:T(8,128)S(1)}, f32[3,2,56,128]{3,2,1,0:T(8,128)S(1)}, f32[3,2,72,128]{3,2,1,0:T(8,128)S(1)}, f32[3,2,72,128]{3,2,1,0:T(...) custom-call(f32[4,2,24,128]{3,2,1,0:T(8,128)S(1)} %get-tuple-element.16.refs_0_, ...), custom_call_target="tpu_custom_call" | custom-call | flops 4000000000 | tf_op jit(solution)/shard_map/fine_chain/pallas_call | solution.py:271
  19.5 2.6 %collective-permute-start.5 = (f32[3,2,52,128]{3,2,1,0:T(8,128)S(1)}, f32[3,2,52,128]{3,2,1,0:T(8,128)S(1)}, u32[]{:S(2)}, u32[]{:S(2)}) collective-permute-start(f32[3,2,52,128]{3,2,1,0:T(8,128)S(1)} %get-tuple-element.27), channel_id=1, source_target_pairs={{0,24},{1,25},{2,26},{3,27},{4,28},{5,29},{6,30},{7,31},{8,16},{9,... | collective-permute-start | bytes 479240 | tf_op jit(solution)/shard_map/ppermute | solution.py:574
  22.1 0.1 settle.1
  22.3 1.2 %collective-permute-start.4 = (f32[3,24,256]{2,1,0:T(8,128)S(1)}, f32[3,24,256]{2,1,0:T(8,128)S(1)}, u32[]{:S(2)}, u32[]{:S(2)}) collective-permute-start(f32[3,24,256]{2,1,0:T(8,128)S(1)} %get-tuple-element.25), channel_id=1, source_target_pairs={{0,16},{1,17},{2,18},{3,19},{4,20},{5,21},{6,22},{7,23},{8,24},{9,... | collective-permute-start | bytes 221192 | tf_op jit(solution)/shard_map/ppermute | solution.py:574
  23.5 3.5 %collective-permute-done.5.refs_2_ = f32[3,2,52,128]{3,2,1,0:T(8,128)S(1)} collective-permute-done((f32[3,2,52,128]{3,2,1,0:T(8,128)S(1)}, f32[3,2,52,128]{3,2,1,0:T(8,128)S(1)}, u32[]{:S(2)}, u32[]{:S(2)}) %collective-permute-start.5) | collective-permute-done | bytes 159776 | tf_op jit(solution)/shard_map/ppermute | solution.py:574
  27.0 2.8 %last_chain.1 = (f32[3,24,256]{2,1,0:T(8,128)S(1)}, f32[3,24,256]{2,1,0:T(8,128)}) custom-call(f32[3,2,56,128]{3,2,1,0:T(8,128)S(1)} %first_link.1.refs_0_, f32[2,88,128]{2,1,0:T(8,128)S(1)} %get-tuple-element.24.refs_4_.refs_1_, f32[3,2,52,128]{3,2,1,0:T(8,128)S(1)} %collective-permute-done.5.refs_2_), custom_call_target="tpu_custom_call" | custom-call | flops 1500000000 | tf_op jit(solution)/shard_map/last_chain/pallas_call | solution.py:271
  29.8 0.0 collective-permute-done.4
  29.8 0.6 %fusion = f32[1,3,24,256]{3,2,1,0:T(8,128)} fusion(f32[3,24,256]{2,1,0:T(8,128)S(1)} %collective-permute-done.4, f32[3,24,256]{2,1,0:T(8,128)S(1)} %get-tuple-element.28, pred[]{:T(512)S(6)} %lt.13), kind=kLoop, calls=%fused_computation.2 | loop fusion | flops 36864 | bytes 221185 | tf_op jit(solution)/shard_map/broadcast_in_dim | solution.py:606
  (3 shorter events, 0.0 us)
Async XLA Ops:
  0.6 0.9 %copy-start = (f32[24,256]{1,0:T(8,128)S(1)}, f32[24,256]{1,0:T(8,128)}, u32[]{:S(2)}) copy-start(f32[24,256]{1,0:T(8,128)} %param.5) | copy-start | bytes 73732
  1.6 8.8 %collective-permute-start.2 = (f32[4,24,256]{2,1,0:T(8,128)S(1)}, f32[4,24,256]{2,1,0:T(8,128)S(1)}, u32[]{:S(2)}, u32[]{:S(2)}) collective-permute-start(f32[4,24,256]{2,1,0:T(8,128)S(1)} %pad_maximum_fusion.refs_0_), channel_id=1, source_target_pairs={{0,6},{1,7},{2,4},{3,5},{4,2},{5,3},{6,0},{7,1},{8,14},{9,15},{10,... | collective-permute-start | bytes 294920 | tf_op jit(solution)/shard_map/ppermute | solution.py:574
  6.7 5.0 %collective-permute-start.1 = (f32[4,24,256]{2,1,0:T(8,128)S(1)}, f32[4,24,256]{2,1,0:T(8,128)S(1)}, u32[]{:S(2)}, u32[]{:S(2)}) collective-permute-start(f32[4,24,256]{2,1,0:T(8,128)S(1)} %pad_maximum_fusion.refs_0_), channel_id=1, source_target_pairs={{0,2},{1,3},{2,0},{3,1},{4,6},{5,7},{6,4},{7,5},{8,10},{9,11},{10,... | collective-permute-start | bytes 294920 | tf_op jit(solution)/shard_map/ppermute | solution.py:574
  6.7 5.1 %collective-permute-start = (f32[4,24,256]{2,1,0:T(8,128)S(1)}, f32[4,24,256]{2,1,0:T(8,128)S(1)}, u32[]{:S(2)}, u32[]{:S(2)}) collective-permute-start(f32[4,24,256]{2,1,0:T(8,128)S(1)} %pad_maximum_fusion.refs_0_), channel_id=1, source_target_pairs={{0,1},{1,0},{2,3},{3,2},{4,5},{5,4},{6,7},{7,6},{8,9},{9,8},{10,11... | collective-permute-start | bytes 294920 | tf_op jit(solution)/shard_map/ppermute | solution.py:574
  11.8 1.4 %collective-permute-start.3 = (f32[4,24,256]{2,1,0:T(8,128)S(1)}, f32[4,24,256]{2,1,0:T(8,128)S(1)}, u32[]{:S(2)}, u32[]{:S(2)}) collective-permute-start(f32[4,24,256]{2,1,0:T(8,128)S(1)} %broadcast_select_fusion), channel_id=1, source_target_pairs={{0,1},{1,0},{2,3},{3,2},{4,5},{5,4},{6,7},{7,6},{8,9},{9,8},{10,11... | collective-permute-start | bytes 294920 | tf_op jit(solution)/shard_map/ppermute | solution.py:574
  19.5 7.5 %collective-permute-start.5 = (f32[3,2,52,128]{3,2,1,0:T(8,128)S(1)}, f32[3,2,52,128]{3,2,1,0:T(8,128)S(1)}, u32[]{:S(2)}, u32[]{:S(2)}) collective-permute-start(f32[3,2,52,128]{3,2,1,0:T(8,128)S(1)} %get-tuple-element.27), channel_id=1, source_target_pairs={{0,24},{1,25},{2,26},{3,27},{4,28},{5,29},{6,30},{7,31},{8,16},{9,... | collective-permute-start | bytes 479240 | tf_op jit(solution)/shard_map/ppermute | solution.py:574
  22.3 7.6 %collective-permute-start.4 = (f32[3,24,256]{2,1,0:T(8,128)S(1)}, f32[3,24,256]{2,1,0:T(8,128)S(1)}, u32[]{:S(2)}, u32[]{:S(2)}) collective-permute-start(f32[3,24,256]{2,1,0:T(8,128)S(1)} %get-tuple-element.25), channel_id=1, source_target_pairs={{0,16},{1,17},{2,18},{3,19},{4,20},{5,21},{6,22},{7,23},{8,24},{9,... | collective-permute-start | bytes 221192 | tf_op jit(solution)/shard_map/ppermute | solution.py:574

commit v4 on v3

--- a/solution.py
+++ b/solution.py
@@ -556,6 +556,23 @@
     )
 
 
+def finish_kernel(standing_at, coarse_ref, fine_ref, got_ref, c_ref, f_ref):
+    early = standing_at[0] < 2
+    strip, columns = coarse_ref.shape[1:]
+    for f in range(3):
+        for b in range(0, strip, BLOCK):
+            for p in range(0, columns, LANES):
+                at = (f, pl.ds(b, BLOCK), pl.ds(p, LANES))
+                got = got_ref[at]
+                c_ref[at] = jnp.where(early, got, coarse_ref[at] + got)
+                f_ref[at] = fine_ref[at]
+
+
+def finish(coarse, fine, got):
+    out = array(*coarse.shape)
+    return call(finish_kernel, "finish", 1, (out, out), [coarse, fine, got])
+
+
 def body(initial_state, c_guess, friction):
     slices, strips = lax.axis_size("tm"), lax.axis_size("space")
     strip = initial_state.shape[1]
@@ -601,8 +618,8 @@
         more = [everyone[: slices - 3, :, :, 2:-2]]
         wide = everyone[slices - 1]
     first = first_link(wide, keep)
-    coarse, f_points = last_chain(first, keep, got_far, more, strip, margin)
-    c_points = jnp.where(which < 2, got, coarse + got)
+    coarse, fine = last_chain(first, keep, got_far, more, strip, margin)
+    c_points, f_points = finish(coarse, fine, got)
     return (c_points[None], f_points[None])
 
 

time: 30.6 us -> 30 us (0.980)
  other arithmetic: 1.57 us -> 0.93 us
    broadcast_in_dim x1 -> x0, other arithmetic: 0.65 us -> none  [body(): return (c_points[None], f_points[None])]
    pallas_call x5 -> x6, Pallas kernels: 9.86 us -> 9.89 us  [call(): pl.pallas_call(lambda *refs: kernel(standing(), *refs), name=name, out_sh...]
  transfers between devices with their start and end apart: 6 -> 6, of which waited for: 4 -> 4; matrix products, arithmetic and copies ran while one was open for 0% -> 0% of each run, Pallas kernels for 11% -> 9%
where the time goes in v4:
time: 30 us; the launch traced here: 29.9 us
  Pallas kernels  9.89 us (33%)
  waiting for transfers between devices  9.33 us (31%)
  starting transfers between devices  9.01 us (30%)
  other arithmetic  0.93 us (3%)
  between operations  0.72 us (2%)
    pallas_call x6, Pallas kernels, call(): pl.pallas_call(lambda *refs: kernel(standing(), *refs), name=name, out_sh...  9.89 us
    ppermute x6, waiting for transfers between devices, moved(): return lax.ppermute(value, both, pairs)  9.33 us
    ppermute x6, starting transfers between devices, moved(): return lax.ppermute(value, both, pairs)  9.01 us
    select_n x1, other arithmetic, body(): start = jnp.where(which >= slices - 2, initial_state, c_guess[0])  0.9 us
  transfers between devices with their start and end apart: 6, of which 4 were waited for; matrix products, arithmetic and copies ran while one was open for 0% of the time, Pallas kernels for 9%

profile of v4, /device:TPU:0, one launch (start us, length us, event | category | flops | bytes accessed | tf_op | source)
XLA Modules:
  0.0 29.9 jit_solution(10355492135588929297)
XLA Ops:
  0.6 0.0 copy-start
  0.6 0.9 %bitcast_select_fusion = f32[3,24,256]{2,1,0:T(8,128)S(1)} fusion(f32[3,24,256]{2,1,0:T(8,128)} %param.3, f32[1,3,24,256]{3,2,1,0:T(8,128)} %param.4, pred[]{:T(512)S(6)} %ge.3), kind=kLoop, calls=%fused_computation.1 | loop fusion | flops 18432 | bytes 221185 | tf_op jit(solution)/shard_map/jit(_where)/select_n | solution.py:596
  1.6 0.0 copy-done
  1.6 5.1 %collective-permute-start.2 = (f32[4,24,256]{2,1,0:T(8,128)S(1)}, f32[4,24,256]{2,1,0:T(8,128)S(1)}, u32[]{:S(2)}, u32[]{:S(2)}) collective-permute-start(f32[4,24,256]{2,1,0:T(8,128)S(1)} %pad_maximum_fusion.refs_0_), channel_id=1, source_target_pairs={{0,6},{1,7},{2,4},{3,5},{4,2},{5,3},{6,0},{7,1},{8,14},{9,15},{10,... | collective-permute-start | bytes 294920 | tf_op jit(solution)/shard_map/ppermute | solution.py:591
  6.7 0.0 collective-permute-start.1
  6.7 0.0 collective-permute-start
  6.7 3.7 %collective-permute-done.2.refs_3_ = f32[4,24,256]{2,1,0:T(8,128)S(1)} collective-permute-done((f32[4,24,256]{2,1,0:T(8,128)S(1)}, f32[4,24,256]{2,1,0:T(8,128)S(1)}, u32[]{:S(2)}, u32[]{:S(2)}) %collective-permute-start.2) | collective-permute-done | bytes 98336 | tf_op jit(solution)/shard_map/ppermute | solution.py:591
  10.4 1.3 %collective-permute-done.1.refs_2_ = f32[4,24,256]{2,1,0:T(8,128)S(1)} collective-permute-done((f32[4,24,256]{2,1,0:T(8,128)S(1)}, f32[4,24,256]{2,1,0:T(8,128)S(1)}, u32[]{:S(2)}, u32[]{:S(2)}) %collective-permute-start.1) | collective-permute-done | bytes 98336 | tf_op jit(solution)/shard_map/ppermute | solution.py:591
  11.8 0.1 collective-permute-start.3
  11.8 0.0 collective-permute-done.refs_1_
  11.9 0.5 %deal.1 = (f32[4,2,24,128]{3,2,1,0:T(8,128)S(1)}, f32[4,2,24,128]{3,2,1,0:T(8,128)S(1)}, f32[4,2,24,128]{3,2,1,0:T(8,128)S(1)}, f32[4,2,24,128]{3,2,1,0:T(8,128)S(1)}) custom-call(f32[4,24,256]{2,1,0:T(8,128)S(1)} %pad_maximum_fusion.refs_0_, f32[4,24,256]{2,1,0:T(8,128)S(1)} %collective-permute-done.refs_1_, ...), custom_call_target="tpu_custom_call" | custom-call | flops 250000000 | tf_op jit(solution)/shard_map/deal/pallas_call | solution.py:271
  12.4 0.8 %collective-permute-done.3.refs_1_ = f32[4,24,256]{2,1,0:T(8,128)S(1)} collective-permute-done((f32[4,24,256]{2,1,0:T(8,128)S(1)}, f32[4,24,256]{2,1,0:T(8,128)S(1)}, u32[]{:S(2)}, u32[]{:S(2)}) %collective-permute-start.3) | collective-permute-done | bytes 98336 | tf_op jit(solution)/shard_map/ppermute | solution.py:591
  13.1 6.4 %fine_chain.1 = (f32[3,2,52,128]{3,2,1,0:T(8,128)S(1)}, f32[3,2,56,128]{3,2,1,0:T(8,128)S(1)}, f32[3,2,72,128]{3,2,1,0:T(8,128)S(1)}, f32[3,2,72,128]{3,2,1,0:T(...) custom-call(f32[4,2,24,128]{3,2,1,0:T(8,128)S(1)} %get-tuple-element.18.refs_0_, ...), custom_call_target="tpu_custom_call" | custom-call | flops 4000000000 | tf_op jit(solution)/shard_map/fine_chain/pallas_call | solution.py:271
  19.5 2.6 %collective-permute-start.4 = (f32[3,2,52,128]{3,2,1,0:T(8,128)S(1)}, f32[3,2,52,128]{3,2,1,0:T(8,128)S(1)}, u32[]{:S(2)}, u32[]{:S(2)}) collective-permute-start(f32[3,2,52,128]{3,2,1,0:T(8,128)S(1)} %get-tuple-element.28), channel_id=1, source_target_pairs={{0,24},{1,25},{2,26},{3,27},{4,28},{5,29},{6,30},{7,31},{8,16},{9,... | collective-permute-start | bytes 479240 | tf_op jit(solution)/shard_map/ppermute | solution.py:591
  22.1 0.1 settle.1
  22.3 1.2 %collective-permute-start.5 = (f32[3,24,256]{2,1,0:T(8,128)S(1)}, f32[3,24,256]{2,1,0:T(8,128)S(1)}, u32[]{:S(2)}, u32[]{:S(2)}) collective-permute-start(f32[3,24,256]{2,1,0:T(8,128)S(1)} %get-tuple-element.31), channel_id=1, source_target_pairs={{0,16},{1,17},{2,18},{3,19},{4,20},{5,21},{6,22},{7,23},{8,24},{9,... | collective-permute-start | bytes 221192 | tf_op jit(solution)/shard_map/ppermute | solution.py:591
  23.5 3.5 %collective-permute-done.4.refs_2_ = f32[3,2,52,128]{3,2,1,0:T(8,128)S(1)} collective-permute-done((f32[3,2,52,128]{3,2,1,0:T(8,128)S(1)}, f32[3,2,52,128]{3,2,1,0:T(8,128)S(1)}, u32[]{:S(2)}, u32[]{:S(2)}) %collective-permute-start.4) | collective-permute-done | bytes 159776 | tf_op jit(solution)/shard_map/ppermute | solution.py:591
  27.0 2.2 %last_chain.1 = (f32[3,24,256]{2,1,0:T(8,128)S(1)}, f32[3,24,256]{2,1,0:T(8,128)S(1)}) custom-call(f32[3,2,56,128]{3,2,1,0:T(8,128)S(1)} %first_link.1.refs_0_, f32[2,88,128]{2,1,0:T(8,128)S(1)} %get-tuple-element.26.refs_4_.refs_1_, f32[3,2,52,128]{3,2,1,0:T(8,128)S(1)} %collective-permute-done.4.refs_2_), custom_call_target="tpu_custom_call" | custom-call | flops 1500000000 | tf_op jit(solution)/shard_map/last_chain/pallas_call | solution.py:271
  29.2 0.0 collective-permute-done.5.refs_2_
  29.2 0.7 %finish.1 = (f32[3,24,256]{2,1,0:T(8,128)}, f32[3,24,256]{2,1,0:T(8,128)}) custom-call(f32[3,24,256]{2,1,0:T(8,128)S(1)} %get-tuple-element.29.refs_0_, f32[3,24,256]{2,1,0:T(8,128)S(1)} %get-tuple-element.30.refs_1_, f32[3,24,256]{2,1,0:T(8,128)S(1)} %collective-permute-done.5.refs_2_), custom_call_target="tpu_custom_call" | custom-call | flops 500000000 | tf_op jit(solution)/shard_map/finish/pallas_call | solution.py:271
  (3 shorter events, 0.0 us)
Async XLA Ops:
  0.6 0.9 %copy-start = (f32[24,256]{1,0:T(8,128)S(1)}, f32[24,256]{1,0:T(8,128)}, u32[]{:S(2)}) copy-start(f32[24,256]{1,0:T(8,128)} %param.5) | copy-start | bytes 73732
  1.6 8.8 %collective-permute-start.2 = (f32[4,24,256]{2,1,0:T(8,128)S(1)}, f32[4,24,256]{2,1,0:T(8,128)S(1)}, u32[]{:S(2)}, u32[]{:S(2)}) collective-permute-start(f32[4,24,256]{2,1,0:T(8,128)S(1)} %pad_maximum_fusion.refs_0_), channel_id=1, source_target_pairs={{0,6},{1,7},{2,4},{3,5},{4,2},{5,3},{6,0},{7,1},{8,14},{9,15},{10,... | collective-permute-start | bytes 294920 | tf_op jit(solution)/shard_map/ppermute | solution.py:591
  6.7 5.0 %collective-permute-start.1 = (f32[4,24,256]{2,1,0:T(8,128)S(1)}, f32[4,24,256]{2,1,0:T(8,128)S(1)}, u32[]{:S(2)}, u32[]{:S(2)}) collective-permute-start(f32[4,24,256]{2,1,0:T(8,128)S(1)} %pad_maximum_fusion.refs_0_), channel_id=1, source_target_pairs={{0,2},{1,3},{2,0},{3,1},{4,6},{5,7},{6,4},{7,5},{8,10},{9,11},{10,... | collective-permute-start | bytes 294920 | tf_op jit(solution)/shard_map/ppermute | solution.py:591
  6.7 5.1 %collective-permute-start = (f32[4,24,256]{2,1,0:T(8,128)S(1)}, f32[4,24,256]{2,1,0:T(8,128)S(1)}, u32[]{:S(2)}, u32[]{:S(2)}) collective-permute-start(f32[4,24,256]{2,1,0:T(8,128)S(1)} %pad_maximum_fusion.refs_0_), channel_id=1, source_target_pairs={{0,1},{1,0},{2,3},{3,2},{4,5},{5,4},{6,7},{7,6},{8,9},{9,8},{10,11... | collective-permute-start | bytes 294920 | tf_op jit(solution)/shard_map/ppermute | solution.py:591
  11.8 1.4 %collective-permute-start.3 = (f32[4,24,256]{2,1,0:T(8,128)S(1)}, f32[4,24,256]{2,1,0:T(8,128)S(1)}, u32[]{:S(2)}, u32[]{:S(2)}) collective-permute-start(f32[4,24,256]{2,1,0:T(8,128)S(1)} %broadcast_select_fusion), channel_id=1, source_target_pairs={{0,1},{1,0},{2,3},{3,2},{4,5},{5,4},{6,7},{7,6},{8,9},{9,8},{10,11... | collective-permute-start | bytes 294920 | tf_op jit(solution)/shard_map/ppermute | solution.py:591
  19.5 7.5 %collective-permute-start.4 = (f32[3,2,52,128]{3,2,1,0:T(8,128)S(1)}, f32[3,2,52,128]{3,2,1,0:T(8,128)S(1)}, u32[]{:S(2)}, u32[]{:S(2)}) collective-permute-start(f32[3,2,52,128]{3,2,1,0:T(8,128)S(1)} %get-tuple-element.28), channel_id=1, source_target_pairs={{0,24},{1,25},{2,26},{3,27},{4,28},{5,29},{6,30},{7,31},{8,16},{9,... | collective-permute-start | bytes 479240 | tf_op jit(solution)/shard_map/ppermute | solution.py:591
  22.3 6.9 %collective-permute-start.5 = (f32[3,24,256]{2,1,0:T(8,128)S(1)}, f32[3,24,256]{2,1,0:T(8,128)S(1)}, u32[]{:S(2)}, u32[]{:S(2)}) collective-permute-start(f32[3,24,256]{2,1,0:T(8,128)S(1)} %get-tuple-element.31), channel_id=1, source_target_pairs={{0,16},{1,17},{2,18},{3,19},{4,20},{5,21},{6,22},{7,23},{8,24},{9,... | collective-permute-start | bytes 221192 | tf_op jit(solution)/shard_map/ppermute | solution.py:591
